TPU v7x, 128 devices: a whole 4x4x4 slice. The times are simulated.
128 devices in a mesh: blk: 16 (over y_hi, x, core), grp: 8 (over y_lo, z).
Axes of the slice: x: 4, y: 4 (y_hi: 2, y_lo: 2; y = y_hi * 2 + y_lo), z: 4, core: 2. Of those that a mesh axis runs over, the one named last changes fastest.
Arguments:
- trial_vec: float32 [6144, 24], P(('blk', 'grp')), may hold values from -6 to 6
- resid_vec: float32 [6144, 24], P(('blk', 'grp')), may hold values from -6 to 6
- search_dir: float32 [6144, 24], P(('blk', 'grp')), may hold values from -6 to 6
- trial_img: float32 [6144, 24], P(('blk', 'grp')), may hold values from -12 to 12
- search_img: float32 [6144, 24], P(('blk', 'grp')), may hold values from -12 to 12
- dens_exch: bfloat16 [6144, 20480], P(('blk', 'grp')), may hold values from -0.078125 to 0.078125
- dens_direct: bfloat16 [6144, 20480], P(('blk', 'grp')), may hold values from -0.078125 to 0.078125
- screen_mat: bfloat16 [20480, 20480], P('grp', 'blk'), may hold values from -0.0390625 to 0.0390625
- coulomb: float32 [20480], replicated, may hold values from 0.2 to 2
- valence_energy: float32 [96], replicated, may hold values from -3 to -1
- conduct_energy: float32 [256], replicated, may hold values from 0.5 to 3
- valence_index: int32 [6144], P(('blk', 'grp')), may hold values from 0 to 95, as said below
- conduct_index: int32 [6144], P(('blk', 'grp')), may hold values from 0 to 255, as said below
- ritz_coef: float32 [72, 24], replicated, may hold values from -1.75 to 1.75
Outputs:
- next_trial: float32 [6144, 24], P(('blk', 'grp'))
- next_trial_img: float32 [6144, 24], P(('blk', 'grp'))
- next_search: float32 [6144, 24], P(('blk', 'grp'))
- next_search_img: float32 [6144, 24], P(('blk', 'grp'))
- gram_matrix: float32 [72, 72], replicated
Inputs may be any that keep to these rules, and one draw needn't show every extreme that they name: `valence_index`: no two pairs have both the same valence band and the same conduction band. `conduct_index`: no two pairs have both the same valence band and the same conduction band.
All inputs are finite; a program needn't handle non-finite values.
Results may differ from a plain program's by a relative error of at most 0.0034.
Values may be sent and summed in bfloat16 or wider, within the bound.
A program may use at most 64 MiB of HBM per device.

v0:
```python
import jax.numpy as jnp
from jax import lax

NE = 24


def tdot(left, right):
    return jnp.dot(left, right, precision=lax.Precision.HIGHEST)


def reference(
    trial_vec,
    resid_vec,
    search_dir,
    trial_img,
    search_img,
    dens_exch,
    dens_direct,
    screen_mat,
    coulomb,
    valence_energy,
    conduct_energy,
    valence_index,
    conduct_index,
    ritz_coef,
):
    gap = (
        conduct_energy[conduct_index.astype(jnp.int32)]
        - valence_energy[valence_index.astype(jnp.int32)]
    )
    resid_half = resid_vec.astype(jnp.bfloat16)
    proj = jnp.dot(dens_exch.T, resid_half, preferred_element_type=jnp.float32)
    weighted = (coulomb[:, None] * proj).astype(jnp.bfloat16)
    exch_term = jnp.dot(dens_exch, weighted, preferred_element_type=jnp.float32)
    seen = jnp.dot(dens_direct.T, resid_half, preferred_element_type=jnp.float32).astype(
        jnp.bfloat16
    )
    screened = jnp.dot(screen_mat, seen, preferred_element_type=jnp.float32).astype(jnp.bfloat16)
    direct_term = jnp.dot(dens_direct, screened, preferred_element_type=jnp.float32)
    resid_img = gap[:, None] * resid_vec + 2.0 * exch_term - direct_term
    basis = jnp.concatenate([trial_vec, resid_vec, search_dir], axis=1)
    images = jnp.concatenate([trial_img, resid_img, search_img], axis=1)
    gram_matrix = tdot(basis.T, images)
    lower = ritz_coef[NE:]
    next_trial = tdot(basis, ritz_coef)
    next_trial_img = tdot(images, ritz_coef)
    next_search = tdot(jnp.concatenate([resid_vec, search_dir], axis=1), lower)
    next_search_img = tdot(jnp.concatenate([resid_img, search_img], axis=1), lower)
    return (next_trial, next_trial_img, next_search, next_search_img, gram_matrix)


def solution(mesh):
    return reference
```

profile of v0, /device:TPU:0, one launch (start us, length us, event | category | flops | bytes accessed | tf_op | source)
XLA Modules:
  0.0 274.0 jit_solution(11607078831989404337)
XLA Ops:
  7.2 0.0 copy-start
  7.2 0.0 all-reduce.8.cloned.1.call-start
  7.2 1.5 copy-done
  8.7 2.4 fusion.17
  11.1 0.0 copy-start.11
  11.1 0.0 copy-start.12
  11.1 0.0 copy-start.4
  11.1 0.0 all-reduce.8.cloned.1.call-update
  11.1 0.6 copy-done.11
  11.8 0.0 copy-done.12
  11.8 0.1 copy-done.4
  11.8 3.3 %fusion.19 = f32[20480,24]{0,1:T(8,128)} fusion(bf16[48,20480]{1,0:T(8,128)(2,1)} %param.11, f32[48,24]{0,1:T(8,128)S(1)} %copy-done.4), kind=kOutput, calls=%fused_computation.31 | convolution fusion | flops 47187072 | bytes 3936768 | tf_op jit(solution)/dot_general | solution.py:35
  15.1 0.0 copy-start.13
  15.1 73.5 %all-reduce.9 = bf16[20480,24]{0,1:T(8,128)(2,1)S(1)} all-reduce(f32[20480,24]{0,1:T(8,128)} %fusion.19), channel_id=2, replica_groups=mesh['axis_0'=128] {'axis_0'}, use_global_device_ids=true, to_apply=%add.1.clone | all-reduce | flops 491520 | bytes 2949120 | tf_op jit(solution)/dot_general | solution.py:35
  88.6 0.0 copy-done.13
  88.6 0.6 dynamic-slice.2
  89.8 0.0 copy-start.10
  89.9 0.0 copy-start.2
  89.9 0.0 copy-start.1
  89.9 0.0 copy-start.5
  89.9 0.0 copy-start.8
  89.9 4.7 %fusion.4 = f32[24,2560]{1,0:T(8,128)S(1)} fusion(bf16[2560,1280]{1,0:T(8,128)(2,1)} %param.12, bf16[20480,24]{0,1:T(8,128)(2,1)S(1)} %all-reduce.9, s32[]{:T(128)} %bitcast.1), kind=kOutput, calls=%fused_computation.10 | convolution fusion | flops 157286400 | bytes 6860804 | tf_op jit(solution)/dot_general | solution.py:38
  94.6 0.0 copy-done.10
  94.6 0.0 copy-start.7
  94.7 0.0 copy-done.2
  94.7 0.8 gather_fusion
  95.5 0.0 copy-done.1
  95.5 0.8 gather_fusion.1
  96.2 0.0 copy-done.5
  96.2 0.0 copy-done.8
  96.3 0.8 fusion.7
  97.1 0.8 fusion.26
  97.8 71.6 %all-reduce.10 = bf16[24,2560]{1,0:T(8,128)(2,1)S(1)} all-reduce(f32[24,2560]{1,0:T(8,128)S(1)} %fusion.4), channel_id=3, replica_groups=[8,16]<=[16,8]T(1,0), use_global_device_ids=true, to_apply=%add.2.clone | all-reduce | flops 61440 | bytes 368640 | tf_op jit(solution)/dot_general | solution.py:38
  169.5 30.3 %all-gather = bf16[24,20480]{1,0:T(8,128)(2,1)S(1)} all-gather(bf16[24,2560]{1,0:T(8,128)(2,1)S(1)} %all-reduce.10), channel_id=4, replica_groups=mesh['axis_0'=16,'axis_1'=8] {'axis_1'}, dimensions={1}, use_global_device_ids=true | all-gather | bytes 1105920 | tf_op jit(solution)/convert_element_type | solution.py:38
  199.7 0.0 all-reduce.8.cloned.1.call-done
  199.7 0.0 copy-done.7
  199.7 0.0 copy-start.3
  199.7 2.3 fusion.2
  202.1 0.0 copy-done.3
  202.1 0.0 copy-start.6
  202.1 0.0 copy-start.9
  202.1 0.6 fusion
  202.7 0.1 copy-done.6
  202.8 0.8 fusion.11
  203.6 0.0 copy-done.9
  203.6 0.2 fusion.5
  203.8 0.8 fusion.6
  204.6 62.5 %all-reduce.3 = f32[72,72]{1,0:T(8,128)} all-reduce(f32[72,72]{1,0:T(8,128)S(1)} %fusion.5), channel_id=5, replica_groups=mesh['axis_0'=128] {'axis_0'}, use_global_device_ids=true, to_apply=%add.3.clone | all-reduce | flops 5184 | bytes 41472 | tf_op jit(solution)/dot_general | solution.py:8
  (7 shorter events, 0.0 us)
Async XLA Ops:
  7.2 1.6 copy-start
  7.2 192.5 %all-reduce.8.cloned.1.call-start = ((), (), s32[]{:S(2)}) async-start(), calls=%async_computation | async-start | bytes 3932160 | tf_op jit(solution)/dot_general | solution.py:32
  11.1 0.7 copy-start.11
  11.1 0.7 copy-start.12
  11.1 0.7 copy-start.4
  15.1 73.5 %copy-start.13 = (u32[128]{0:T(128)S(1)}, u32[128]{0:T(128)}, u32[]{:S(2)}) copy-start(u32[128]{0:T(128)} %constant.18) | copy-start | bytes 1540
  89.8 4.8 %copy-start.10 = (f32[48,24]{0,1:T(8,128)S(1)}, f32[48,24]{0,1:T(8,128)}, u32[]{:S(2)}) copy-start(f32[48,24]{0,1:T(8,128)} %param) | copy-start | bytes 13828
  89.9 4.8 %copy-start.2 = (f32[256]{0:T(256)S(1)}, f32[256]{0:T(256)}, u32[]{:S(2)}) copy-start(f32[256]{0:T(256)} %param.5) | copy-start | bytes 3076
  89.9 5.6 %copy-start.1 = (f32[96]{0:T(128)S(1)}, f32[96]{0:T(128)}, u32[]{:S(2)}) copy-start(f32[96]{0:T(128)} %param.7) | copy-start | bytes 1156
  89.9 6.4 %copy-start.5 = (f32[72,24]{0,1:T(8,128)S(1)}, f32[72,24]{0,1:T(8,128)}, u32[]{:S(2)}) copy-start(f32[72,24]{0,1:T(8,128)} %param.3) | copy-start | bytes 20740
  89.9 6.4 %copy-start.8 = (f32[48,24]{0,1:T(8,128)S(1)}, f32[48,24]{0,1:T(8,128)}, u32[]{:S(2)}) copy-start(f32[48,24]{0,1:T(8,128)} %param.2) | copy-start | bytes 13828
  94.6 105.1 %copy-start.7 = (f32[20480]{0:T(1024)S(1)}, f32[20480]{0:T(1024)}, u32[]{:S(2)}) copy-start(f32[20480]{0:T(1024)} %param.9) | copy-start | bytes 245764
  199.7 2.3 copy-start.3
  202.1 0.7 copy-start.6
  202.1 1.5 copy-start.9
Sparse Core Ops, SparseCore 0:
  12.8 153.9 all-reduce.7
where the time goes:
time: 275 us; the launch traced here: 274 us
  blocking collectives  238 us (87%)
  matrix products  16.7 us (6%)
  between operations  14.9 us (5%)
  local copies, waits for them, and re-layouts  4.48 us (2%)
    dot_general x1, blocking collectives, reference(): jnp.dot(dens_direct.T, resid_half, preferred_element_type=jnp.float32)  73.5 us
    dot_general x1, blocking collectives, reference(): jnp.dot(screen_mat, seen, preferred_element_type=jnp.float32)  71.6 us
    dot_general x1, blocking collectives, tdot(): return jnp.dot(left, right, precision=lax.Precision.HIGHEST)  62.5 us
    convert_element_type x1, blocking collectives, reference(): jnp.dot(screen_mat, seen, preferred_element_type=jnp.float32)  30.3 us
  transfers between devices with their start and end apart: 1, of which 0 were waited for; matrix products, arithmetic and copies ran while one was open for 4% of the time, Pallas kernels for 0%

commit v1 on v0

v1 whole, which is shorter than its diff:
```python
import jax
import jax.numpy as jnp
from jax import lax
from jax.experimental import pallas as pl
from jax.experimental.pallas import tpu as pltpu
from jax.sharding import PartitionSpec as P

NE = 24
ROWS = 48
NG = 20480
COLS = 640
MESH = pl.DeviceIdType.MESH
FAR = (2, 1, 3)
F32 = jnp.float32
BF16 = jnp.bfloat16
X, R, S = (pl.ds(i * NE, NE) for i in range(3))


NT = ((1,), (1,))


def exact(a, b, dims=((1,), (0,))):
    return lax.dot_general(
        a, b, (dims, ((), ())), precision=lax.Precision.HIGHEST, preferred_element_type=F32
    )


def nt(a, b):
    return lax.dot_general(a, b, (((1,), (1,)), ((), ())), preferred_element_type=F32)


def nn(a, b):
    return lax.dot_general(a, b, (((1,), (0,)), ((), ())), preferred_element_type=F32)


def kernel(
    trial_h, resid_h, search_h, trial_img_h, search_img_h, dens_e_h, dens_d_h, screen_h,
    coulomb_h, val_e_h, con_e_h, val_i_h, con_i_h, ritz_h,
    o_trial, o_trial_img, o_search, o_search_img, o_gram,
    basis, images, dens_e, dens_d, screen, coulomb, val_e, con_e, val_i, con_i, ritz,
    rt, s0s, s0r, acc, s1s, s1r, s2s, s2r, s3s, s3r,
    seen, bacc, c0s, c0r, c1s, c1r, c2s, c2r, gat, early, late,
    ld, s0x, s0y, s1x, s1y, s2x, s2y, s3x, s3y, s4x, s4y,
    c0x, c0y, c1x, c1y, c2x, c2y, a1x, a1y, a2x, a2y, a3x, a3y, ex, ey, lx, ly,
):
    blk = lax.axis_index("blk")
    grp = lax.axis_index("grp")
    c = blk % 2
    x = (blk // 2) % 4
    y_hi = blk // 8
    y_lo = grp // 4
    z = grp % 4
    y = y_hi * 2 + y_lo
    at = {"x": x, "y": y, "z": z}

    def device(x=x, y=y, z=z, c=c):
        return ((y // 2) * 8 + x * 2 + c, (y % 2) * 4 + z)

    def along(axis, step):
        return device(**{axis: (at[axis] + step) % 4})

    other = device(c=1 - c)

    loads = []
    for i, (src, dst) in enumerate((
        (resid_h, basis.at[R]), (dens_d_h, dens_d), (dens_e_h, dens_e), (screen_h, screen),
        (trial_h, basis.at[X]), (search_h, basis.at[S]), (trial_img_h, images.at[X]),
        (search_img_h, images.at[S]), (coulomb_h, coulomb), (val_e_h, val_e), (con_e_h, con_e),
        (val_i_h, val_i), (con_i_h, con_i), (ritz_h, ritz),
    )):
        copy = pltpu.make_async_copy(src, dst, ld.at[i])
        copy.start()
        loads.append(copy)

    barrier = pltpu.get_barrier_semaphore()
    peers = [other] + [along(a, d) for a in "xyz" for d in FAR]
    for peer in peers:
        pl.semaphore_signal(barrier, inc=1, device_id=peer, device_id_type=MESH)

    sends = []

    def send(src, dst, ssem, rsem, dev):
        copy = pltpu.make_async_remote_copy(
            src_ref=src, dst_ref=dst, send_sem=ssem, recv_sem=rsem,
            device_id=dev, device_id_type=MESH,
        )
        copy.start()
        sends.append(copy)

    def landed(ref, rsem, ssem):
        pltpu.make_async_remote_copy(
            src_ref=ref, dst_ref=ref, send_sem=ssem, recv_sem=rsem,
            device_id=other, device_id_type=MESH,
        ).wait_recv()

    STEPS = FAR + (0,)
    dens = (dens_d, dens_e)
    first = ("x", "z")
    third = ("z", "x")

    def lanes(block):
        return pl.ds(pl.multiple_of(block * COLS, COLS), COLS)

    def part_block(p, step1, step2, core):
        a1 = (at[first[p]] + step1) % 4
        a2 = (y + step2) % 4
        return (a2 // 2) * 16 + a1 * 4 + core * 2 + a2 % 2

    loads[0].wait()
    rt[...] = basis[R, :].astype(BF16)

    def core_parts(p):
        loads[1 + p].wait()
        for k in range(4):
            for j in range(4):
                block = part_block(p, STEPS[k], STEPS[j], 1 - c)
                s0s[p, k, j] = nn(rt[...], dens[p][:, lanes(block)]).astype(BF16)
            if p == 0 and k == 0:
                pl.semaphore_wait(barrier, len(peers))
            send(s0s.at[p, k], s0r.at[p, k], s0x.at[p, k], s0y.at[p, k], other)

    def own_parts(p):
        for k in range(4):
            for j in range(4):
                block = part_block(p, STEPS[k], STEPS[j], c)
                acc[p, k, j] = nn(rt[...], dens[p][:, lanes(block)])

    def first_axis(p):
        for k in range(4):
            landed(s0r.at[p, k], s0y.at[p, k], s0x.at[p, k])
            for j in range(4):
                v = acc[p, k, j] + s0r[p, k, j].astype(F32)
                if k == 3:
                    acc[p, k, j] = v
                else:
                    s1s[p, k, j] = v.astype(BF16)
                    send(s1s.at[p, k, j], s1r.at[p, k, j], s1x.at[p, k, j], s1y.at[p, k, j],
                         along(first[p], STEPS[k]))

    def second_axis(p):
        for j in range(4):
            v = acc[p, 3, j]
            for k in range(3):
                landed(s1r.at[p, k, j], s1y.at[p, k, j], s1x.at[p, k, j])
                v = v + s1r[p, k, j].astype(F32)
            if j == 3:
                acc[p, 3, j] = v
            else:
                s2s[p, j] = v.astype(BF16)
                send(s2s.at[p, j], s2r.at[p, j], s2x.at[p, j], s2y.at[p, j], along("y", STEPS[j]))

    def third_axis(p):
        v = acc[p, 3, 3]
        for j in range(3):
            landed(s2r.at[p, j], s2y.at[p, j], s2x.at[p, j])
            v = v + s2r[p, j].astype(F32)
        acc[p, 3, 3] = v
        s3s[p] = v.astype(BF16)
        for k in range(3):
            send(s3s.at[p], s3r.at[p, k], s3x.at[p, k], s3y.at[p, k], along(third[p], FAR[k]))

    def total(p):
        v = acc[p, 3, 3]
        for k in range(3):
            landed(s3r.at[p, k], s3y.at[p, k], s3x.at[p, k])
            v = v + s3r[p, k].astype(F32)
        return v

    BACK = (0,) + FAR

    def gat_block(p, stepy, stepz, core):
        yy = (y + 4 - stepy) % 4
        zz = (z + 4 - stepz) % 4
        if p == 0:
            return ((yy % 2) * 4 + zz) * 4 + core * 2 + yy // 2
        return (yy // 2) * 16 + zz * 4 + core * 2 + yy % 2

    def pass_on(p, m, kz, block):
        ref = gat.at[p, block]
        if m == 0 and kz == 0:
            for k in range(3):
                send(ref, ref, a1x.at[p, k], a1y.at[p, k], along("y", FAR[k]))
        if kz == 0:
            for k in range(3):
                send(ref, ref, a2x.at[p, k, m], a2y.at[p, k, m], along("z", FAR[k]))
        send(ref, ref, a3x.at[p, kz, m], a3y.at[p, kz, m], other)

    def use(p, block):
        return nt(gat[p, block], dens[p][:, lanes(block)])

    def gather_mine(p, term):
        block = gat_block(p, 0, 0, c)
        pass_on(p, 0, 0, block)
        part = use(p, block)
        return part if term is None else term + part

    def gather_y(p, term):
        for m in range(1, 4):
            block = gat_block(p, BACK[m], 0, c)
            landed(gat.at[p, block], a1y.at[p, m - 1], a1x.at[p, m - 1])
            pass_on(p, m, 0, block)
            term = term + use(p, block)
        return term

    def gather_z(p, term):
        for m in range(4):
            for kz in range(1, 4):
                block = gat_block(p, BACK[m], BACK[kz], c)
                landed(gat.at[p, block], a2y.at[p, kz - 1, m], a2x.at[p, kz - 1, m])
                pass_on(p, m, kz, block)
                term = term + use(p, block)
        return term

    def gather_core(p, term):
        for m in range(4):
            for kz in range(4):
                block = gat_block(p, BACK[m], BACK[kz], 1 - c)
                landed(gat.at[p, block], a3y.at[p, kz, m], a3x.at[p, kz, m])
                term = term + use(p, block)
        return term

    def share(buf, ssem, rsem, s, value):
        axis = "cxyz"[s]
        count = 2 if axis == "c" else 4
        here = c if axis == "c" else at[axis]
        buf[s, here] = value
        for k in range(count - 1):
            dev = other if axis == "c" else along(axis, FAR[k])
            send(buf.at[s, here], buf.at[s, here], ssem.at[s, k], rsem.at[s, here], dev)

    def shared(buf, ssem, rsem, s):
        axis = "cxyz"[s]
        count = 2 if axis == "c" else 4
        here = c if axis == "c" else at[axis]
        for k in range(count - 1):
            there = 1 - c if axis == "c" else (here + FAR[k]) % 4
            landed(buf.at[s, there], rsem.at[s, there], ssem.at[s, k])
        value = buf[s, 0]
        for i in range(1, count):
            value = value + buf[s, i]
        return value

    with jax.named_scope("core_d"):
        core_parts(0)
    with jax.named_scope("own_d"):
        own_parts(0)
    with jax.named_scope("first_d"):
        first_axis(0)
    with jax.named_scope("core_e"):
        core_parts(1)
    with jax.named_scope("own_e"):
        own_parts(1)
    with jax.named_scope("first_e"):
        first_axis(1)
    with jax.named_scope("early"):
        for i in (4, 5, 6, 7, 9, 10, 11, 12, 13):
            loads[i].wait()
        share(early, ex, ey, 0, jnp.concatenate(
            [exact(images[X, :], basis[...], NT), exact(images[S, :], basis[...], NT)], axis=0))
    with jax.named_scope("second_d"):
        second_axis(0)
    with jax.named_scope("second_e"):
        second_axis(1)
    with jax.named_scope("third_d"):
        third_axis(0)
    with jax.named_scope("third_e"):
        third_axis(1)
    share(early, ex, ey, 1, shared(early, ex, ey, 0))

    with jax.named_scope("seen"):
        tot = total(0)
        seen[y_lo] = tot.astype(BF16)
        send(seen.at[y_lo], seen.at[y_lo], s4x, s4y, along("y", 5 - 2 * y_lo))
    with jax.named_scope("mm_near"):
        loads[3].wait()
        for q in range(4):
            bacc[q] = nt(seen[y_lo], screen[pl.ds(q * COLS, COLS), lanes(y_lo)])

    with jax.named_scope("weighted"):
        tot = total(1)
        loads[8].wait()
        mine = gat_block(1, 0, 0, c)
        gat[1, mine] = (coulomb[:, lanes(mine)] * tot).astype(BF16)
        exch = gather_mine(1, None)

    def rest(q):
        rows = pl.ds(pl.multiple_of(q * COLS, COLS), COLS)
        return bacc[q] + nt(seen[1 - y_lo], screen[rows, lanes(1 - y_lo)])

    with jax.named_scope("mm_far"):
        landed(seen.at[1 - y_lo], s4y, s4x)
        for i in range(2):
            c0s[i] = rest((1 - c) * 2 + i).astype(BF16)
            send(c0s.at[i], c0r.at[i], c0x.at[i], c0y.at[i], other)
        away = rest(c * 2 + 1 - y_hi)
        home = rest(c * 2 + y_hi)

    with jax.named_scope("c0"):
        for i in range(2):
            landed(c0r.at[i], c0y.at[i], c0x.at[i])
        c1s[...] = (away + c0r[1 - y_hi].astype(F32)).astype(BF16)
        send(c1s, c1r, c1x, c1y, along("y", 2))
        home = home + c0r[y_hi].astype(F32)

    share(early, ex, ey, 2, shared(early, ex, ey, 1))
    with jax.named_scope("gather_y_e"):
        exch = gather_y(1, exch)

    with jax.named_scope("c1"):
        landed(c1r, c1y, c1x)
        home = home + c1r[...].astype(F32)
        c2s[...] = home.astype(BF16)
        for k in range(3):
            send(c2s, c2r.at[k], c2x.at[k], c2y.at[k], along("x", FAR[k]))

    share(early, ex, ey, 3, shared(early, ex, ey, 2))
    with jax.named_scope("gather_z_e"):
        exch = gather_z(1, exch)

    with jax.named_scope("c2"):
        for k in range(3):
            landed(c2r.at[k], c2y.at[k], c2x.at[k])
            home = home + c2r[k].astype(F32)
        mine = gat_block(0, 0, 0, c)
        gat[0, mine] = home.astype(BF16)
        direct = gather_mine(0, None)

    with jax.named_scope("gather_core_e"):
        exch = gather_core(1, exch)

    with jax.named_scope("plain"):
        def pick(energy, index, count):
            hot = (lax.broadcasted_iota(jnp.int32, (count, ROWS), 0) == index[...]).astype(F32)
            return exact(energy[...], hot)

        gap = pick(con_e, con_i, con_e.shape[1]) - pick(val_e, val_i, val_e.shape[1])
        near = gap * basis[R, :] + 2.0 * exch
        all_coef = ritz[...]
        column = lax.broadcasted_iota(jnp.int32, all_coef.shape, 1)
        lower = jnp.where(column >= NE, all_coef, 0.0)
        o_trial[...] = exact(all_coef, basis[...])
        o_search[...] = exact(lower, basis[...])

    with jax.named_scope("gather_y_d"):
        direct = gather_y(0, direct)
    gram = shared(early, ex, ey, 3)
    with jax.named_scope("gather_z_d"):
        direct = gather_z(0, direct)
    with jax.named_scope("gather_core_d"):
        direct = gather_core(0, direct)

    with jax.named_scope("image"):
        resid_img = near - direct
        share(late, lx, ly, 0, exact(resid_img, basis[...], NT))
        images[R, :] = resid_img
        o_trial_img[...] = exact(all_coef, images[...])
        o_search_img[...] = exact(lower, images[...])
    for s in range(1, 4):
        with jax.named_scope(f"late{s}"):
            share(late, lx, ly, s, shared(late, lx, ly, s - 1))
    with jax.named_scope("late4"):
        mid = shared(late, lx, ly, 3)
        gram = jnp.concatenate([gram[0:NE], mid, gram[NE:2 * NE]], axis=0)
        o_gram[...] = jnp.transpose(gram)

    with jax.named_scope("drain"):
        for copy in sends:
            copy.wait_send()


def put(*refs):
    n = len(refs) // 2
    sem = refs[-1]
    copies = [pltpu.make_async_copy(refs[i], refs[n + i], sem.at[i]) for i in range(n)]
    for copy in copies:
        copy.start()
    for copy in copies:
        copy.wait()


def solution(mesh):
    def body(trial, resid, search, trial_img, search_img, dens_e, dens_d, screen,
             coulomb, val_e, con_e, val_i, con_i, ritz):
        args = (trial.T, resid.T, search.T, trial_img.T, search_img.T, dens_e, dens_d, screen,
                coulomb.reshape(1, -1), val_e.reshape(1, -1), con_e.reshape(1, -1),
                val_i.reshape(1, -1), con_i.reshape(1, -1), ritz.T)
        dma = pltpu.SemaphoreType.DMA
        block = (NE, COLS)
        tall = pltpu.VMEM((3 * NE, ROWS), F32)
        scratch = [tall, tall] + [pltpu.VMEM(a.shape, a.dtype) for a in args[5:]] + [
            pltpu.VMEM((NE, ROWS), BF16),
            pltpu.VMEM((2, 4, 4) + block, BF16),
            pltpu.VMEM((2, 4, 4) + block, BF16),
            pltpu.VMEM((2, 4, 4) + block, F32),
            pltpu.VMEM((2, 3, 4) + block, BF16),
            pltpu.VMEM((2, 3, 4) + block, BF16),
            pltpu.VMEM((2, 3) + block, BF16),
            pltpu.VMEM((2, 3) + block, BF16),
            pltpu.VMEM((2,) + block, BF16),
            pltpu.VMEM((2, 3) + block, BF16),
            pltpu.VMEM((2,) + block, BF16),
            pltpu.VMEM((4,) + block, F32),
            pltpu.VMEM((2,) + block, BF16),
            pltpu.VMEM((2,) + block, BF16),
            pltpu.VMEM(block, BF16),
            pltpu.VMEM(block, BF16),
            pltpu.VMEM(block, BF16),
            pltpu.VMEM((3,) + block, BF16),
            pltpu.VMEM((2, 32) + block, BF16),
            pltpu.VMEM((4, 4, 2 * NE, 3 * NE), F32),
            pltpu.VMEM((4, 4, NE, 3 * NE), F32),
            dma((14,)),
            dma((2, 4)), dma((2, 4)),
            dma((2, 3, 4)), dma((2, 3, 4)),
            dma((2, 3)), dma((2, 3)),
            dma((2, 3)), dma((2, 3)),
            dma, dma,
            dma((2,)), dma((2,)),
            dma, dma,
            dma((3,)), dma((3,)),
            dma((2, 3)), dma((2, 3)),
            dma((2, 3, 4)), dma((2, 3, 4)),
            dma((2, 4, 4)), dma((2, 4, 4)),
            dma((4, 3)), dma((4, 4)),
            dma((4, 3)), dma((4, 4)),
        ]
        vec = jax.ShapeDtypeStruct((NE, ROWS), F32)
        outs = (vec, vec, vec, vec, jax.ShapeDtypeStruct((3 * NE, 3 * NE), F32))
        parts = pl.pallas_call(
            kernel,
            out_shape=outs,
            in_specs=[pl.BlockSpec(memory_space=pl.ANY)] * len(args),
            out_specs=[pl.BlockSpec(memory_space=pltpu.VMEM)] * 5,
            scratch_shapes=scratch,
            compiler_params=pltpu.CompilerParams(
                collective_id=0, has_side_effects=True, vmem_limit_bytes=67043328
            ),
            name="step",
        )(*args)
        parts = pl.pallas_call(
            put,
            out_shape=outs,
            in_specs=[pl.BlockSpec(memory_space=pltpu.VMEM)] * 5,
            out_specs=[pl.BlockSpec(memory_space=pl.ANY)] * 5,
            scratch_shapes=[dma((5,))],
            name="put",
        )(*parts)
        return tuple(a.T for a in parts[:4]) + (parts[4],)

    both = P(("blk", "grp"), None)
    one = P(("blk", "grp"))
    return jax.shard_map(
        body,
        mesh=mesh,
        in_specs=(both,) * 7 + (P("grp", "blk"), P(None), P(None), P(None), one, one, P(None, None)),
        out_specs=(both,) * 4 + (P(None, None),),
        check_vma=False,
    )
```

time: 275 us -> 64.2 us (0.23)
  blocking collectives: 238 us -> 0 us
  Pallas kernels: 0 us -> 63.4 us
  matrix products: 16.7 us -> 0 us
  between operations: 14.9 us -> 0.65 us
  local copies, waits for them, and re-layouts: 4.48 us -> 0 us
    dot_general x3 -> x0, blocking collectives: 208 us -> none  [the longest x1 73.5 us: reference(): jnp.dot(dens_direct.T, resid_half, preferred_element_type=jnp.float32)]
    pallas_call x0 -> x2, Pallas kernels: none -> 63.4 us  [the longest x1 61.9 us: body(): pl.pallas_call(kernel, out_shape=outs, in_specs=[pl.BlockSpec(memory_spac...]
    convert_element_type x1 -> x0, blocking collectives: 30.3 us -> none  [reference(): jnp.dot(screen_mat, seen, preferred_element_type=jnp.float32)]
    dot_general x10 -> x0, matrix products: 16.7 us -> none  [the longest x1 4.7 us: reference(): jnp.dot(screen_mat, seen, preferred_element_type=jnp.float32)]
  transfers between devices with their start and end apart: 1 -> 0, of which waited for: 0 -> 0; matrix products, arithmetic and copies ran while one was open for 4% -> 0% of each run, Pallas kernels for 0% -> 0%
where the time goes in v1:
time: 64.2 us; the launch traced here: 64 us
  Pallas kernels  63.4 us (99%)
  between operations  0.65 us (1%)
    pallas_call x1, Pallas kernels, body(): pl.pallas_call(kernel, out_shape=outs, in_specs=[pl.BlockSpec(memory_spac...  61.9 us
    pallas_call x1, Pallas kernels, body(): pl.pallas_call(put, out_shape=outs, in_specs=[pl.BlockSpec(memory_space=p...  1.51 us

profile of v1, /device:TPU:0, one launch (start us, length us, event | category | flops | bytes accessed | tf_op | source)
XLA Modules:
  0.0 64.0 jit_solution(13520711027151036202)
XLA Ops:
  0.6 61.9 %step.1 = (f32[24,48]{1,0:T(8,128)}, f32[24,48]{1,0:T(8,128)}, f32[24,48]{1,0:T(8,128)}, f32[24,48]{1,0:T(8,128)}, f32[72,72]{1,0:T(8,128)}) custom-call(f32[24,48]{1,0:T(8,128)} %bitcast.16, f32[24,48]{1,0:T(8,128)} %bitcast.17, f32[24,48]{1,0:T(8,128)} %bitcast.18, f32[24,48]{1,0:T(8,128)} %bitcast.19, f32[24,48]{1,0:T(8,128)} %bitcast.20, ...), custom_call_target="tpu_custom_call" | custom-call | tf_op jit(solution)/shard_map/step/pallas_call | solution.py:429
  62.5 1.5 %put.1 = (f32[24,48]{1,0:T(8,128)}, f32[24,48]{1,0:T(8,128)}, f32[24,48]{1,0:T(8,128)}, f32[24,48]{1,0:T(8,128)}, f32[72,72]{1,0:T(8,128)}) custom-call(f32[24,48]{1,0:T(8,128)} %get-tuple-element.15.refs_0_, f32[24,48]{1,0:T(8,128)} %get-tuple-element.16.refs_1_, f32[24,48]{1,0:T(8,128)} %get-tuple-element.17.refs_2_, f32[24,48]{1,0:T(8,128)} %get-tuple-element.18.refs_3_, ...), custom_call_target="tpu_custom_call" | custom-call | tf_op jit(solution)/shard_map/put/pallas_call | solution.py:440

commit v2 on v1

v2 whole, which is shorter than its diff:
```python
import jax
import jax.numpy as jnp
from jax import lax
from jax.experimental import pallas as pl
from jax.experimental.pallas import tpu as pltpu
from jax.sharding import PartitionSpec as P

NE = 24
ROWS = 48
NG = 20480
COLS = 640
MESH = pl.DeviceIdType.MESH
FAR = (2, 1, 3)
F32 = jnp.float32
BF16 = jnp.bfloat16
X, R, S = (pl.ds(i * NE, NE) for i in range(3))


NT = ((1,), (1,))


def exact(a, b, dims=((1,), (0,))):
    return lax.dot_general(
        a, b, (dims, ((), ())), precision=lax.Precision.HIGHEST, preferred_element_type=F32
    )


def nt(a, b):
    return lax.dot_general(a, b, (((1,), (1,)), ((), ())), preferred_element_type=F32)


def nn(a, b):
    return lax.dot_general(a, b, (((1,), (0,)), ((), ())), preferred_element_type=F32)


def kernel(
    trial_h, resid_h, search_h, trial_img_h, search_img_h, dens_e_h, dens_d_h, screen_h,
    coulomb_h, val_e_h, con_e_h, val_i_h, con_i_h, ritz_h,
    h_trial, h_trial_img, h_search, h_search_img, h_gram,
    o_trial, o_trial_img, o_search, o_search_img, o_gram,
    basis, images, dens_e, dens_d, screen, coulomb, val_e, con_e, val_i, con_i, ritz,
    rt, s0s, s0r, acc, rls, rlr, s1s, s1r, s2s, s2r, s3s, s3r,
    qb, seen, bacc, c0s, c0r, c1s, c1r, c2s, c2r, gat, early, late,
    ld, st, sx, ex, lx, s0y, s0q, rly, rlq, s1y, s1q, s2y, s3y, s4y, c0y, c1y, c2y,
    a1y, a2y, a3y, ey, ly,
):
    blk = lax.axis_index("blk")
    grp = lax.axis_index("grp")
    c = blk % 2
    x = (blk // 2) % 4
    y_hi = blk // 8
    y_lo = grp // 4
    z = grp % 4
    y = y_hi * 2 + y_lo
    at = {"x": x, "y": y, "z": z}

    def device(x=x, y=y, z=z, c=c):
        return ((y // 2) * 8 + x * 2 + c, (y % 2) * 4 + z)

    def along(axis, step):
        return device(**{axis: (at[axis] + step) % 4})

    other = device(c=1 - c)

    loads = []
    for i, (src, dst) in enumerate((
        (resid_h, basis.at[R]), (dens_d_h, dens_d), (dens_e_h, dens_e), (screen_h, screen),
        (trial_h, basis.at[X]), (search_h, basis.at[S]), (trial_img_h, images.at[X]),
        (search_img_h, images.at[S]), (coulomb_h, coulomb), (val_e_h, val_e), (con_e_h, con_e),
        (val_i_h, val_i), (con_i_h, con_i), (ritz_h, ritz),
    )):
        copy = pltpu.make_async_copy(src, dst, ld.at[i])
        copy.start()
        loads.append(copy)

    barrier = pltpu.get_barrier_semaphore()
    peers = [other] + [along(a, d) for a in "xyz" for d in FAR]
    for peer in peers:
        pl.semaphore_signal(barrier, inc=1, device_id=peer, device_id_type=MESH)

    stores = []

    def store(i, src, dst):
        copy = pltpu.make_async_copy(src, dst, st.at[i])
        copy.start()
        stores.append(copy)

    def send(src, dst, ssem, rsem, dev):
        copy = pltpu.make_async_remote_copy(
            src_ref=src, dst_ref=dst, send_sem=ssem, recv_sem=rsem,
            device_id=dev, device_id_type=MESH,
        )
        copy.start()

    def landed(ref, rsem):
        pltpu.make_async_remote_copy(
            src_ref=ref, dst_ref=ref, send_sem=sx.at[0], recv_sem=rsem,
            device_id=other, device_id_type=MESH,
        ).wait_recv()

    def left(ref, ssem):
        pltpu.make_async_remote_copy(
            src_ref=ref, dst_ref=ref, send_sem=ssem, recv_sem=s4y,
            device_id=other, device_id_type=MESH,
        ).wait_send()

    STEPS = FAR + (0,)
    dens = (dens_d, dens_e, dens_d, dens_d, dens_d)
    group = (R, R, X, R, S)
    first = ("x", "z", "z", "z", "z")
    second = ("y",) * 5
    third = ("z", "x")

    def lanes(block):
        return pl.ds(pl.multiple_of(block * COLS, COLS), COLS)

    def part_block(p, step1, step2, core):
        a1 = (at[first[p]] + step1) % 4
        a2 = (at[second[p]] + step2) % 4
        if p == 0:
            return (a2 // 2) * 16 + a1 * 4 + core * 2 + a2 % 2
        if p == 1:
            return core * 16 + a2 * 4 + a1
        return ((a2 % 2) * 4 + a1) * 4 + core * 2 + a2 // 2

    loads[0].wait()
    rt[R, :] = basis[R, :].astype(BF16)

    def core_parts(p):
        if p < 2:
            loads[1 + p].wait()
        for k in range(4):
            for j in range(4):
                block = part_block(p, STEPS[k], STEPS[j], 1 - c)
                s0s[p, k, j] = nn(rt[group[p], :], dens[p][:, lanes(block)]).astype(BF16)
            if p == 0 and k == 0:
                pl.semaphore_wait(barrier, len(peers))
            send(s0s.at[p, k], s0r.at[p, k], sx.at[0], s0y.at[p, k] if p < 2 else s0q.at[p - 2], other)

    def own_parts(p):
        for k in range(4):
            for j in range(4):
                block = part_block(p, STEPS[k], STEPS[j], c)
                acc[p, k, j] = nn(rt[group[p], :], dens[p][:, lanes(block)])

    def first_axis(p):
        if p > 1:
            landed(s0r.at[p], s0q.at[p - 2])
        for k in range(4):
            if p < 2:
                landed(s0r.at[p, k], s0y.at[p, k])
            for j in range(4):
                v = acc[p, k, j] + s0r[p, k, j].astype(F32)
                if k == 0:
                    rls[p, j] = v.astype(BF16)
                    send(rls.at[p, j], rlr.at[p, j], sx.at[1], rly.at[p, j] if p < 2 else rlq.at[p - 2],
                         along(first[p], 1 if j < 2 else 3))
                elif k == 1 and j >= 2:
                    ring(p, 0, j, v)
                elif k == 2 and j < 2:
                    ring(p, 1, j, v)
                else:
                    acc[p, k, j] = v

    def ring(p, way, j, v):
        s1s[p, way, j] = v.astype(BF16)
        send(s1s.at[p, way, j], s1r.at[p, way, j], sx.at[2],
             s1y.at[p, way, j] if p < 2 else s1q.at[p - 2], along(first[p], (1, 3)[way]))

    def relay(p):
        if p > 1:
            landed(rlr.at[p], rlq.at[p - 2])
        for j in (0, 2, 1, 3):
            way = 0 if j < 2 else 1
            if p < 2:
                landed(rlr.at[p, j], rly.at[p, j])
            ring(p, way, j, acc[p, 1 + way, j] + rlr[p, j].astype(F32))

    def second_axis(p):
        for j in (0, 2, 1, 3):
            v = acc[p, 3, j]
            for way in range(2):
                landed(s1r.at[p, way, j], s1y.at[p, way, j])
                v = v + s1r[p, way, j].astype(F32)
            if j == 3:
                acc[p, 3, j] = v
            else:
                s2s[p, j] = v.astype(BF16)
                send(s2s.at[p, j], s2r.at[p, j], sx.at[3], s2y.at[p], along(second[p], STEPS[j]))

    def gram_rows(p):
        landed(s1r.at[p], s1q.at[p - 2])
        for j in range(4):
            v = acc[p, 3, j]
            for way in range(2):
                v = v + s1r[p, way, j].astype(F32)
            qb[j, group[p], :] = v.astype(BF16)

    def third_axis(p):
        v = acc[p, 3, 3]
        landed(s2r.at[p], s2y.at[p])
        for j in range(3):
            v = v + s2r[p, j].astype(F32)
        acc[p, 3, 3] = v
        s3s[p] = v.astype(BF16)
        for k in range(3):
            send(s3s.at[p], s3r.at[p, k], sx.at[4], s3y.at[p], along(third[p], FAR[k]))

    def total(p):
        v = acc[p, 3, 3]
        landed(s3r.at[p], s3y.at[p])
        for k in range(3):
            v = v + s3r[p, k].astype(F32)
        return v

    BACK = (0,) + FAR
    BACKZ = (0, 1, 3, 2)
    row = ("y", "y")
    col = ("z", "z")

    def gat_block(p, m, kz, core):
        g1 = (at[row[p]] + 4 - BACK[m]) % 4
        g2 = (at[col[p]] + 4 - BACKZ[kz]) % 4
        if p == 0:
            return ((g1 % 2) * 4 + g2) * 4 + core * 2 + g1 // 2
        return core * 16 + g1 * 4 + g2

    def pass_on(p, m, kz):
        ref = gat.at[p, gat_block(p, m, kz, c)]
        send(ref, ref, sx.at[9 + p], a3y.at[p, min(kz, 1)], other)
        if m == 0 and kz == 0:
            for k in range(3):
                send(ref, ref, sx.at[9 + p], a1y.at[p, k], along(row[p], FAR[k]))
        if (kz == 0 and m % 2 == 1) or (kz == 2 and m % 2 == 0):
            send(ref, ref, sx.at[9 + p], a2y.at[p, 2, m], along(col[p], 2 if kz == 0 else 3))
        if kz == 0:
            for way in range(2):
                send(ref, ref, sx.at[9 + p], a2y.at[p, way, m], along(col[p], (1, 3)[way]))

    def use(p, core, pairs):
        term = None
        for m, kz in pairs:
            block = gat_block(p, m, kz, core)
            part = nt(gat[p, block], dens[p][:, lanes(block)])
            term = part if term is None else term + part
        return term

    ROW = [(m, 0) for m in range(4)]
    REST = [(m, kz) for kz in (1, 2) for m in range(4)] + [(m, 3) for m in range(4)]

    def gather_y(p):
        for m in (2, 3, 1):
            landed(gat.at[p, gat_block(p, m, 0, c)], a1y.at[p, m - 1])
            pass_on(p, m, 0)

    def gather_near(p):
        for m in (0, 2, 3, 1):
            for kz in (2, 1):
                landed(gat.at[p, gat_block(p, m, kz, c)], a2y.at[p, kz - 1, m])
                pass_on(p, m, kz)

    def gather_far(p, which):
        for m in which:
            landed(gat.at[p, gat_block(p, m, 3, c)], a2y.at[p, 2, m])
            pass_on(p, m, 3)

    def gather_core(p, rest):
        landed(gat.at[p, pl.ds(0, 12 if rest else 4)], a3y.at[p, rest])

    def share(buf, ssem, rsem, s, value):
        axis = "cxyz"[s]
        count = 2 if axis == "c" else 4
        here = c if axis == "c" else at[axis]
        buf[s, here] = value
        for k in range(count - 1):
            dev = other if axis == "c" else along(axis, FAR[k])
            send(buf.at[s, here], buf.at[s, here], ssem.at[s], rsem.at[s], dev)

    def shared(buf, rsem, s):
        count = 2 if s == 0 else 4
        landed(buf.at[s, pl.ds(0, count - 1)], rsem.at[s])
        value = buf[s, 0]
        for i in range(1, count):
            value = value + buf[s, i]
        return value

    scope = jax.named_scope
    with scope("core_d"):
        core_parts(0)
    with scope("own_d"):
        own_parts(0)
    with scope("first_d"):
        first_axis(0)
    with scope("core_e"):
        core_parts(1)
    with scope("own_e"):
        own_parts(1)
    with scope("first_e"):
        first_axis(1)
    with scope("q_x"):
        for i in (4, 5):
            loads[i].wait()
        rt[X, :] = basis[X, :].astype(BF16)
        rt[S, :] = basis[S, :].astype(BF16)
        core_parts(2)
    with scope("relay_d"):
        relay(0)
    with scope("relay_e"):
        own_parts(2)
        relay(1)
    with scope("first_x"):
        first_axis(2)
        core_parts(3)
    with scope("second_d"):
        second_axis(0)
    with scope("early"):
        for i in (6, 7, 9, 10, 11, 12, 13):
            loads[i].wait()
        share(early, ex, ey, 0, jnp.concatenate(
            [exact(images[X, :], basis[...], NT), exact(images[S, :], basis[...], NT)], axis=0))
        own_parts(3)
    with scope("second_e"):
        second_axis(1)
    with scope("third_d"):
        third_axis(0)
    with scope("first_r"):
        first_axis(3)
        relay(2)
        core_parts(4)
        own_parts(4)
    with scope("third_e"):
        third_axis(1)

    with scope("early1"):
        share(early, ex, ey, 1, shared(early, ey, 0))

    with scope("seen"):
        tot = total(0)
        seen[y_lo] = tot.astype(BF16)
        send(seen.at[y_lo], seen.at[y_lo], sx.at[5], s4y, along("y", 5 - 2 * y_lo))
    with scope("mm_near"):
        loads[3].wait()
        for q in range(4):
            bacc[q] = nt(seen[y_lo], screen[pl.ds(q * COLS, COLS), lanes(y_lo)])
    with scope("first_s"):
        relay(3)
        first_axis(4)
    with scope("weighted"):
        tot = total(1)
        loads[8].wait()
        mine = gat_block(1, 0, 0, c)
        gat[1, mine] = (coulomb[:, lanes(mine)] * tot).astype(BF16)
    with scope("mm_far"):
        landed(seen.at[1 - y_lo], s4y)
        kept = []
        for i in (1, 0, 3, 2):
            core = c if i > 1 else 1 - c
            half = y_hi if i in (0, 2) else 1 - y_hi
            q = core * 2 + half
            rows = pl.ds(pl.multiple_of(q * COLS, COLS), COLS)
            v = bacc[q] + nt(seen[1 - y_lo], screen[rows, lanes(1 - y_lo)])
            if i > 1:
                kept.append(v)
            else:
                c0s[i] = v.astype(BF16)
                send(c0s.at[i], c0r.at[i], sx.at[6], c0y.at[i], other)
        away, home = kept
        pass_on(1, 0, 0)
    with scope("rows_x"):
        gram_rows(2)

    with scope("c0"):
        for i in (1, 0):
            landed(c0r.at[i], c0y.at[i])
            if i == 1:
                c1s[...] = (away + c0r[1].astype(F32)).astype(BF16)
                send(c1s, c1r, sx.at[7], c1y, along("y", 2))
            else:
                home = home + c0r[0].astype(F32)
    with scope("relay_s"):
        relay(4)
        share(early, ex, ey, 2, shared(early, ey, 1))
    with scope("gather_y_e"):
        gather_y(1)
        exch = use(1, c, ROW)
        gram_rows(3)

    with scope("c1"):
        landed(c1r, c1y)
        home = home + c1r[...].astype(F32)
        c2s[...] = home.astype(BF16)
        for k in range(3):
            send(c2s, c2r.at[k], sx.at[8], c2y, along("x", FAR[k]))

    with scope("plain"):
        def pick(energy, index, count):
            hot = (lax.broadcasted_iota(jnp.int32, (count, ROWS), 0) == index[...]).astype(F32)
            return exact(energy[...], hot)

        gap = pick(con_e, con_i, con_e.shape[1]) - pick(val_e, val_i, val_e.shape[1])
        all_coef = ritz[...]
        column = lax.broadcasted_iota(jnp.int32, all_coef.shape, 1)
        lower = jnp.where(column >= NE, all_coef, 0.0)
        o_trial[...] = exact(all_coef, basis[...])
        o_search[...] = exact(lower, basis[...])
        store(0, o_trial, h_trial)
        store(1, o_search, h_search)
        gram_rows(4)
    with scope("gather_near_e"):
        gather_near(1)

    with scope("c2"):
        landed(c2r, c2y)
        for k in range(3):
            home = home + c2r[k].astype(F32)
        gat[0, gat_block(0, 0, 0, c)] = home.astype(BF16)
        pass_on(0, 0, 0)

    with scope("gather_far_e"):
        gather_far(1, (0, 2, 3, 1))
        exch = exch + use(1, c, REST)
    with scope("gather_y_d"):
        gather_y(0)
    with scope("gather_core_e"):
        gather_core(1, 0)
        gather_core(1, 1)
        exch = exch + use(1, 1 - c, ROW + REST)
        near = gap * basis[R, :] + 2.0 * exch
        late_near = exact(near, basis[...], NT)

    with scope("gram_d"):
        part = None
        for m, j in ((0, 3), (1, 0), (2, 2), (3, 1)):
            term = nt(gat[0, gat_block(0, m, 0, c)], qb[j])
            part = term if part is None else part + term
        share(late, lx, ly, 0, late_near - part)
        direct = use(0, c, ROW)
    with scope("early3"):
        share(early, ex, ey, 3, shared(early, ey, 2))
    with scope("core_row_d"):
        gather_core(0, 0)
        direct = direct + use(0, 1 - c, ROW)
    with scope("late1"):
        share(late, lx, ly, 1, shared(late, ly, 0))
    with scope("gather_near_d"):
        gather_near(0)
    with scope("gather_far_d"):
        gather_far(0, (0, 2))
    with scope("late2"):
        share(late, lx, ly, 2, shared(late, ly, 1))
    with scope("gather_far2_d"):
        gather_far(0, (3, 1))
    with scope("rest_d"):
        direct = direct + use(0, c, REST)
        gram = shared(early, ey, 3)
    with scope("gather_core_d"):
        gather_core(0, 1)
        direct = direct + use(0, 1 - c, REST)
    with scope("late3"):
        share(late, lx, ly, 3, shared(late, ly, 2))
    with scope("image"):
        images[R, :] = near - direct
        o_trial_img[...] = exact(all_coef, images[...])
        o_search_img[...] = exact(lower, images[...])
        store(2, o_trial_img, h_trial_img)
        store(3, o_search_img, h_search_img)
    with scope("late4"):
        mid = shared(late, ly, 3)
        gram = jnp.concatenate([gram[0:NE], mid, gram[NE:2 * NE]], axis=0)
        o_gram[...] = jnp.transpose(gram)
        store(4, o_gram, h_gram)

    with jax.named_scope("drain"):
        for i, ref in enumerate((
            s0s, rls, s1s, s2s, s3r, seen.at[0], c0s, c1s, c2r,
            gat.at[0, pl.ds(0, 31)], gat.at[1, pl.ds(0, 31)],
        )):
            left(ref, sx.at[i])
        for i in range(4):
            count = 1 if i == 0 else 3
            left(early.at[i, pl.ds(0, count)], ex.at[i])
            left(late.at[i, pl.ds(0, count)], lx.at[i])
        for copy in stores:
            copy.wait()


def put(*refs):
    n = len(refs) // 2
    sem = refs[-1]
    copies = [pltpu.make_async_copy(refs[i], refs[n + i], sem.at[i]) for i in range(n)]
    for copy in copies:
        copy.start()
    for copy in copies:
        copy.wait()


def solution(mesh):
    def body(trial, resid, search, trial_img, search_img, dens_e, dens_d, screen,
             coulomb, val_e, con_e, val_i, con_i, ritz):
        args = (trial.T, resid.T, search.T, trial_img.T, search_img.T, dens_e, dens_d, screen,
                coulomb.reshape(1, -1), val_e.reshape(1, -1), con_e.reshape(1, -1),
                val_i.reshape(1, -1), con_i.reshape(1, -1), ritz.T)
        dma = pltpu.SemaphoreType.DMA
        block = (NE, COLS)
        tall = pltpu.VMEM((3 * NE, ROWS), F32)
        flat = pltpu.VMEM((NE, ROWS), F32)
        scratch = [flat, flat, flat, flat, pltpu.VMEM((3 * NE, 3 * NE), F32), tall, tall] + [pltpu.VMEM(a.shape, a.dtype) for a in args[5:]] + [
            pltpu.VMEM((3 * NE, ROWS), BF16),
            pltpu.VMEM((5, 4, 4) + block, BF16),
            pltpu.VMEM((5, 4, 4) + block, BF16),
            pltpu.VMEM((5, 4, 4) + block, F32),
            pltpu.VMEM((5, 4) + block, BF16),
            pltpu.VMEM((5, 4) + block, BF16),
            pltpu.VMEM((5, 2, 4) + block, BF16),
            pltpu.VMEM((5, 2, 4) + block, BF16),
            pltpu.VMEM((2, 3) + block, BF16),
            pltpu.VMEM((2, 3) + block, BF16),
            pltpu.VMEM((2,) + block, BF16),
            pltpu.VMEM((2, 3) + block, BF16),
            pltpu.VMEM((4, 3 * NE, COLS), BF16),
            pltpu.VMEM((2,) + block, BF16),
            pltpu.VMEM((4,) + block, F32),
            pltpu.VMEM((2,) + block, BF16),
            pltpu.VMEM((2,) + block, BF16),
            pltpu.VMEM(block, BF16),
            pltpu.VMEM(block, BF16),
            pltpu.VMEM(block, BF16),
            pltpu.VMEM((3,) + block, BF16),
            pltpu.VMEM((2, 32) + block, BF16),
            pltpu.VMEM((4, 4, 2 * NE, 3 * NE), F32),
            pltpu.VMEM((4, 4, NE, 3 * NE), F32),
            dma((14,)), dma((5,)), dma((11,)), dma((4,)), dma((4,)),
            dma((2, 4)), dma((3,)), dma((2, 4)), dma((3,)), dma((2, 2, 4)), dma((3,)),
            dma((2,)), dma((2,)), dma, dma((2,)), dma, dma,
            dma((2, 3)), dma((2, 3, 4)), dma((2, 2)), dma((4,)), dma((4,)),
        ]
        vec = jax.ShapeDtypeStruct((NE, ROWS), F32)
        outs = (vec, vec, vec, vec, jax.ShapeDtypeStruct((3 * NE, 3 * NE), F32))
        parts = pl.pallas_call(
            kernel,
            out_shape=outs,
            in_specs=[pl.BlockSpec(memory_space=pl.ANY)] * len(args),
            out_specs=[pl.BlockSpec(memory_space=pl.ANY)] * 5,
            scratch_shapes=scratch,
            compiler_params=pltpu.CompilerParams(
                collective_id=0, has_side_effects=True, vmem_limit_bytes=67043328
            ),
            name="step",
        )(*args)
        parts = pl.pallas_call(
            put,
            out_shape=outs,
            in_specs=[pl.BlockSpec(memory_space=pltpu.VMEM)] * 5,
            out_specs=[pl.BlockSpec(memory_space=pl.ANY)] * 5,
            scratch_shapes=[dma((5,))],
            compiler_params=pltpu.CompilerParams(vmem_limit_bytes=67043328),
            name="put",
        )(*parts)
        return tuple(a.T for a in parts[:4]) + (parts[4],)

    both = P(("blk", "grp"), None)
    one = P(("blk", "grp"))
    return jax.shard_map(
        body,
        mesh=mesh,
        in_specs=(both,) * 7 + (P("grp", "blk"), P(None), P(None), P(None), one, one, P(None, None)),
        out_specs=(both,) * 4 + (P(None, None),),
        check_vma=False,
    )
```

time: 64.2 us -> 57.2 us (0.89)
  Pallas kernels: 63.4 us -> 56.4 us
    pallas_call x1, Pallas kernels: 61.9 us -> 54.9 us  [body(): pl.pallas_call(kernel, out_shape=outs, in_specs=[pl.BlockSpec(memory_spac...]
where the time goes in v2:
time: 57.2 us; the launch traced here: 57 us
  Pallas kernels  56.4 us (99%)
  between operations  0.65 us (1%)
    pallas_call x1, Pallas kernels, body(): pl.pallas_call(kernel, out_shape=outs, in_specs=[pl.BlockSpec(memory_spac...  54.9 us
    pallas_call x1, Pallas kernels, body(): pl.pallas_call(put, out_shape=outs, in_specs=[pl.BlockSpec(memory_space=p...  1.51 us

profile of v2, /device:TPU:0, one launch (start us, length us, event | category | flops | bytes accessed | tf_op | source)
XLA Modules:
  0.0 57.0 jit_solution(1294590382436714561)
XLA Ops:
  0.6 54.9 %step.1 = (f32[24,48]{1,0:T(8,128)}, f32[24,48]{1,0:T(8,128)}, f32[24,48]{1,0:T(8,128)}, f32[24,48]{1,0:T(8,128)}, f32[72,72]{1,0:T(8,128)}) custom-call(f32[24,48]{1,0:T(8,128)} %bitcast.16, f32[24,48]{1,0:T(8,128)} %bitcast.17, f32[24,48]{1,0:T(8,128)} %bitcast.18, f32[24,48]{1,0:T(8,128)} %bitcast.19, f32[24,48]{1,0:T(8,128)} %bitcast.20, ...), custom_call_target="tpu_custom_call" | custom-call | tf_op jit(solution)/shard_map/step/pallas_call | solution.py:539
  55.5 1.5 %put.1 = (f32[24,48]{1,0:T(8,128)}, f32[24,48]{1,0:T(8,128)}, f32[24,48]{1,0:T(8,128)}, f32[24,48]{1,0:T(8,128)}, f32[72,72]{1,0:T(8,128)}) custom-call(f32[24,48]{1,0:T(8,128)} %get-tuple-element.15.refs_0_, f32[24,48]{1,0:T(8,128)} %get-tuple-element.16.refs_1_, f32[24,48]{1,0:T(8,128)} %get-tuple-element.17.refs_2_, f32[24,48]{1,0:T(8,128)} %get-tuple-element.18.refs_3_, ...), custom_call_target="tpu_custom_call" | custom-call | tf_op jit(solution)/shard_map/put/pallas_call | solution.py:550

commit v3 on v2

--- a/solution.py
+++ b/solution.py
@@ -36,12 +36,11 @@
 def kernel(
     trial_h, resid_h, search_h, trial_img_h, search_img_h, dens_e_h, dens_d_h, screen_h,
     coulomb_h, val_e_h, con_e_h, val_i_h, con_i_h, ritz_h,
-    h_trial, h_trial_img, h_search, h_search_img, h_gram,
     o_trial, o_trial_img, o_search, o_search_img, o_gram,
     basis, images, dens_e, dens_d, screen, coulomb, val_e, con_e, val_i, con_i, ritz,
     rt, s0s, s0r, acc, rls, rlr, s1s, s1r, s2s, s2r, s3s, s3r,
     qb, seen, bacc, c0s, c0r, c1s, c1r, c2s, c2r, gat, early, late,
-    ld, st, sx, ex, lx, s0y, s0q, rly, rlq, s1y, s1q, s2y, s3y, s4y, c0y, c1y, c2y,
+    ld, sx, s0y, s0q, rly, rlq, s1y, s1q, s2y, s3y, s4y, c0y, c1y, c2y,
     a1y, a2y, a3y, ey, ly,
 ):
     blk = lax.axis_index("blk")
@@ -52,7 +51,7 @@
     y_lo = grp // 4
     z = grp % 4
     y = y_hi * 2 + y_lo
-    at = {"x": x, "y": y, "z": z}
+    at = {"x": x, "y": y, "z": z, "c": c}
 
     def device(x=x, y=y, z=z, c=c):
         return ((y // 2) * 8 + x * 2 + c, (y % 2) * 4 + z)
@@ -65,25 +64,27 @@
     loads = []
     for i, (src, dst) in enumerate((
         (resid_h, basis.at[R]), (dens_d_h, dens_d), (dens_e_h, dens_e), (screen_h, screen),
-        (trial_h, basis.at[X]), (search_h, basis.at[S]), (trial_img_h, images.at[X]),
-        (search_img_h, images.at[S]), (coulomb_h, coulomb), (val_e_h, val_e), (con_e_h, con_e),
-        (val_i_h, val_i), (con_i_h, con_i), (ritz_h, ritz),
+        (coulomb_h, coulomb), (val_e_h, val_e), (con_e_h, con_e), (val_i_h, val_i),
+        (con_i_h, con_i), (ritz_h, ritz),
     )):
         copy = pltpu.make_async_copy(src, dst, ld.at[i])
         copy.start()
         loads.append(copy)
+    for i, (src, dst) in enumerate((
+        (trial_h, basis.at[X]), (search_h, basis.at[S]),
+        (trial_img_h, images.at[X]), (search_img_h, images.at[S]),
+    )):
+        pltpu.make_async_copy(src, dst, ld.at[10 + i // 2]).start()
+
+    def pair_done(buf, sem):
+        two = buf.at[pl.ds(0, 2 * NE)]
+        pltpu.make_async_copy(two, two, sem).wait()
 
     barrier = pltpu.get_barrier_semaphore()
     peers = [other] + [along(a, d) for a in "xyz" for d in FAR]
+    peers += [device(x=(x + d) % 4, c=1 - c) for d in FAR]
     for peer in peers:
         pl.semaphore_signal(barrier, inc=1, device_id=peer, device_id_type=MESH)
-
-    stores = []
-
-    def store(i, src, dst):
-        copy = pltpu.make_async_copy(src, dst, st.at[i])
-        copy.start()
-        stores.append(copy)
 
     def send(src, dst, ssem, rsem, dev):
         copy = pltpu.make_async_remote_copy(
@@ -135,7 +136,7 @@
                 s0s[p, k, j] = nn(rt[group[p], :], dens[p][:, lanes(block)]).astype(BF16)
             if p == 0 and k == 0:
                 pl.semaphore_wait(barrier, len(peers))
-            send(s0s.at[p, k], s0r.at[p, k], sx.at[0], s0y.at[p, k] if p < 2 else s0q.at[p - 2], other)
+            send(s0s.at[p, k], s0r.at[p, k], sx.at[0], s0q.at[p - 2] if p > 1 else s0y.at[p, k], other)
 
     def own_parts(p):
         for k in range(4):
@@ -146,26 +147,33 @@
     def first_axis(p):
         if p > 1:
             landed(s0r.at[p], s0q.at[p - 2])
-        for k in range(4):
+
+        def chunk(k):
             if p < 2:
                 landed(s0r.at[p, k], s0y.at[p, k])
-            for j in range(4):
-                v = acc[p, k, j] + s0r[p, k, j].astype(F32)
-                if k == 0:
-                    rls[p, j] = v.astype(BF16)
-                    send(rls.at[p, j], rlr.at[p, j], sx.at[1], rly.at[p, j] if p < 2 else rlq.at[p - 2],
-                         along(first[p], 1 if j < 2 else 3))
-                elif k == 1 and j >= 2:
-                    ring(p, 0, j, v)
-                elif k == 2 and j < 2:
-                    ring(p, 1, j, v)
-                else:
-                    acc[p, k, j] = v
+
+        def both(k, j):
+            return acc[p, k, j] + s0r[p, k, j].astype(F32)
+
+        chunk(0)
+        for j in (0, 2, 1, 3):
+            rls[p, j] = both(0, j).astype(BF16)
+            send(rls.at[p, j], rlr.at[p, j], sx.at[1], rlq.at[p - 2] if p > 1 else rly.at[p, j],
+                 along(first[p], 1 if j < 2 else 3))
+        chunk(1)
+        chunk(2)
+        for k, j in ((1, 2), (2, 0), (1, 3), (2, 1)):
+            ring(p, k - 1, j, both(k, j))
+        for k, j in ((1, 0), (2, 2), (1, 1), (2, 3)):
+            acc[p, k, j] = both(k, j)
+        chunk(3)
+        for j in range(4):
+            acc[p, 3, j] = both(3, j)
 
     def ring(p, way, j, v):
         s1s[p, way, j] = v.astype(BF16)
-        send(s1s.at[p, way, j], s1r.at[p, way, j], sx.at[2],
-             s1y.at[p, way, j] if p < 2 else s1q.at[p - 2], along(first[p], (1, 3)[way]))
+        send(s1s.at[p, way, j], s1r.at[p, way, j], sx.at[1],
+             s1q.at[p - 2] if p > 1 else s1y.at[p, way, j], along(first[p], (1, 3)[way]))
 
     def relay(p):
         if p > 1:
@@ -186,7 +194,7 @@
                 acc[p, 3, j] = v
             else:
                 s2s[p, j] = v.astype(BF16)
-                send(s2s.at[p, j], s2r.at[p, j], sx.at[3], s2y.at[p], along(second[p], STEPS[j]))
+                send(s2s.at[p, j], s2r.at[p, j], sx.at[2], s2y.at[p], along(second[p], STEPS[j]))
 
     def gram_rows(p):
         landed(s1r.at[p], s1q.at[p - 2])
@@ -203,8 +211,8 @@
             v = v + s2r[p, j].astype(F32)
         acc[p, 3, 3] = v
         s3s[p] = v.astype(BF16)
-        for k in range(3):
-            send(s3s.at[p], s3r.at[p, k], sx.at[4], s3y.at[p], along(third[p], FAR[k]))
+        for k in (0, 2, 1):
+            send(s3s.at[p], s3r.at[p, k], sx.at[2], s3y.at[p], along(third[p], FAR[k]))
 
     def total(p):
         v = acc[p, 3, 3]
@@ -227,15 +235,16 @@
 
     def pass_on(p, m, kz):
         ref = gat.at[p, gat_block(p, m, kz, c)]
-        send(ref, ref, sx.at[9 + p], a3y.at[p, min(kz, 1)], other)
+        send(ref, ref, sx.at[3], a3y.at[p, min(kz, 1)], other)
         if m == 0 and kz == 0:
-            for k in range(3):
-                send(ref, ref, sx.at[9 + p], a1y.at[p, k], along(row[p], FAR[k]))
+            for k in (0, 2, 1):
+                send(ref, ref, sx.at[3], a1y.at[p, k], along(row[p], FAR[k]))
+        if kz == 0:
+            send(ref, ref, sx.at[3], a2y.at[p, 1, m], along(col[p], 3))
         if (kz == 0 and m % 2 == 1) or (kz == 2 and m % 2 == 0):
-            send(ref, ref, sx.at[9 + p], a2y.at[p, 2, m], along(col[p], 2 if kz == 0 else 3))
+            send(ref, ref, sx.at[3], a2y.at[p, 2, m], along(col[p], 2 if kz == 0 else 3))
         if kz == 0:
-            for way in range(2):
-                send(ref, ref, sx.at[9 + p], a2y.at[p, way, m], along(col[p], (1, 3)[way]))
+            send(ref, ref, sx.at[3], a2y.at[p, 0, m], along(col[p], 1))
 
     def use(p, core, pairs):
         term = None
@@ -267,22 +276,88 @@
     def gather_core(p, rest):
         landed(gat.at[p, pl.ds(0, 12 if rest else 4)], a3y.at[p, rest])
 
-    def share(buf, ssem, rsem, s, value):
+    HALF = (pl.ds(0, 384), pl.ds(384, 256))
+    ROWS2 = ("y", "z")
+    COLS2 = ("z", "y")
+
+    def d_block(h, m, kz, core):
+        g1 = (at[ROWS2[h]] + 4 - BACK[m]) % 4
+        g2 = (at[COLS2[h]] + 4 - BACKZ[kz]) % 4
+        yy, zz = (g1, g2) if h == 0 else (g2, g1)
+        return ((yy % 2) * 4 + zz) * 4 + core * 2 + yy // 2
+
+    def d_ref(h, m, kz):
+        return gat.at[0, d_block(h, m, kz, c), :, HALF[h]]
+
+    def d_row():
+        for k in (0, 2, 1):
+            for h in range(2):
+                ref = d_ref(h, 0, 0)
+                send(ref, ref, sx.at[4 + h], a1y.at[2 * h, k], along(ROWS2[h], FAR[k]))
+
+    def d_pass(h, m, kz):
+        ref = d_ref(h, m, kz)
+        ssem = sx.at[4 + h]
+        send(ref, ref, ssem, a3y.at[0, h], other)
+        if kz == 0:
+            send(ref, ref, ssem, a2y.at[2 * h, 1, m], along(COLS2[h], 3))
+        if (kz == 0 and m < 2) or (kz == 2 and m > 1):
+            send(ref, ref, ssem, a2y.at[2 * h, 2, m], along(COLS2[h], 2 if kz == 0 else 3))
+        if kz == 0:
+            send(ref, ref, ssem, a2y.at[2 * h, 0, m], along(COLS2[h], 1))
+
+    def d_gather_row():
+        for m in (2, 3, 1):
+            for h in range(2):
+                landed(d_ref(h, m, 0), a1y.at[2 * h, m - 1])
+                d_pass(h, m, 0)
+
+    def d_gather_near(which):
+        for m in which:
+            for h in range(2):
+                for kz in (2, 1):
+                    landed(d_ref(h, m, kz), a2y.at[2 * h, kz - 1, m])
+                    d_pass(h, m, kz)
+
+    def d_gather_far(which):
+        for m in which:
+            for h in range(2):
+                landed(d_ref(h, m, 3), a2y.at[2 * h, 2, m])
+                d_pass(h, m, 3)
+
+    def spread(buf, sem, ssem, here, value, devices):
+        buf[here] = value
+        for dev in devices:
+            send(buf.at[here], buf.at[here], ssem, sem, dev)
+
+    def collected(buf, sem, count):
+        landed(buf.at[pl.ds(0, count - 1)], sem)
+        value = buf[0]
+        for i in range(1, count):
+            value = value + buf[i]
+        return value
+
+    def share_early(s, value):
         axis = "cxyz"[s]
-        count = 2 if axis == "c" else 4
-        here = c if axis == "c" else at[axis]
-        buf[s, here] = value
-        for k in range(count - 1):
-            dev = other if axis == "c" else along(axis, FAR[k])
-            send(buf.at[s, here], buf.at[s, here], ssem.at[s], rsem.at[s], dev)
-
-    def shared(buf, rsem, s):
-        count = 2 if s == 0 else 4
-        landed(buf.at[s, pl.ds(0, count - 1)], rsem.at[s])
-        value = buf[s, 0]
-        for i in range(1, count):
-            value = value + buf[s, i]
-        return value
+        devices = [other] if s == 0 else [along(axis, d) for d in FAR]
+        spread(early.at[s], ey.at[s], sx.at[6 if s == 0 else 7], at[axis], value, devices)
+
+    def early_sum(s):
+        return collected(early.at[s], ey.at[s], 4 if s else 2)
+
+    LATE = (pl.ds(0, 8), pl.ds(8, 4), pl.ds(12, 4))
+
+    def share_late(s, value):
+        if s == 0:
+            devices = [other] + [device(x=(x + d) % 4, c=k) for k in (1 - c, c) for d in (2, 3, 1)]
+            here = x * 2 + c
+        else:
+            devices = [along("xyz"[s], d) for d in (2, 3, 1)]
+            here = at["xyz"[s]]
+        spread(late.at[LATE[s]], ly.at[s], sx.at[8 if s == 0 else 9], here, value, devices)
+
+    def late_sum(s):
+        return collected(late.at[LATE[s]], ly.at[s], 4 if s else 8)
 
     scope = jax.named_scope
     with scope("core_d"):
@@ -298,8 +373,7 @@
     with scope("first_e"):
         first_axis(1)
     with scope("q_x"):
-        for i in (4, 5):
-            loads[i].wait()
+        pair_done(basis, ld.at[10])
         rt[X, :] = basis[X, :].astype(BF16)
         rt[S, :] = basis[S, :].astype(BF16)
         core_parts(2)
@@ -314,9 +388,10 @@
     with scope("second_d"):
         second_axis(0)
     with scope("early"):
-        for i in (6, 7, 9, 10, 11, 12, 13):
+        pair_done(images, ld.at[11])
+        for i in range(5, 10):
             loads[i].wait()
-        share(early, ex, ey, 0, jnp.concatenate(
+        share_early(0, jnp.concatenate(
             [exact(images[X, :], basis[...], NT), exact(images[S, :], basis[...], NT)], axis=0))
         own_parts(3)
     with scope("second_e"):
@@ -332,12 +407,12 @@
         third_axis(1)
 
     with scope("early1"):
-        share(early, ex, ey, 1, shared(early, ey, 0))
+        share_early(1, early_sum(0))
 
     with scope("seen"):
         tot = total(0)
         seen[y_lo] = tot.astype(BF16)
-        send(seen.at[y_lo], seen.at[y_lo], sx.at[5], s4y, along("y", 5 - 2 * y_lo))
+        send(seen.at[y_lo], seen.at[y_lo], sx.at[2], s4y, along("y", 5 - 2 * y_lo))
     with scope("mm_near"):
         loads[3].wait()
         for q in range(4):
@@ -347,7 +422,7 @@
         first_axis(4)
     with scope("weighted"):
         tot = total(1)
-        loads[8].wait()
+        loads[4].wait()
         mine = gat_block(1, 0, 0, c)
         gat[1, mine] = (coulomb[:, lanes(mine)] * tot).astype(BF16)
     with scope("mm_far"):
@@ -363,7 +438,7 @@
                 kept.append(v)
             else:
                 c0s[i] = v.astype(BF16)
-                send(c0s.at[i], c0r.at[i], sx.at[6], c0y.at[i], other)
+                send(c0s.at[i], c0r.at[i], sx.at[2], c0y.at[i], other)
         away, home = kept
         pass_on(1, 0, 0)
     with scope("rows_x"):
@@ -374,12 +449,12 @@
             landed(c0r.at[i], c0y.at[i])
             if i == 1:
                 c1s[...] = (away + c0r[1].astype(F32)).astype(BF16)
-                send(c1s, c1r, sx.at[7], c1y, along("y", 2))
+                send(c1s, c1r, sx.at[2], c1y, along("y", 2))
             else:
                 home = home + c0r[0].astype(F32)
     with scope("relay_s"):
         relay(4)
-        share(early, ex, ey, 2, shared(early, ey, 1))
+        share_early(2, early_sum(1))
     with scope("gather_y_e"):
         gather_y(1)
         exch = use(1, c, ROW)
@@ -389,8 +464,8 @@
         landed(c1r, c1y)
         home = home + c1r[...].astype(F32)
         c2s[...] = home.astype(BF16)
-        for k in range(3):
-            send(c2s, c2r.at[k], sx.at[8], c2y, along("x", FAR[k]))
+        for k in (0, 2, 1):
+            send(c2s, c2r.at[k], sx.at[2], c2y, along("x", FAR[k]))
 
     with scope("plain"):
         def pick(energy, index, count):
@@ -403,8 +478,6 @@
         lower = jnp.where(column >= NE, all_coef, 0.0)
         o_trial[...] = exact(all_coef, basis[...])
         o_search[...] = exact(lower, basis[...])
-        store(0, o_trial, h_trial)
-        store(1, o_search, h_search)
         gram_rows(4)
     with scope("gather_near_e"):
         gather_near(1)
@@ -414,74 +487,64 @@
         for k in range(3):
             home = home + c2r[k].astype(F32)
         gat[0, gat_block(0, 0, 0, c)] = home.astype(BF16)
-        pass_on(0, 0, 0)
+        d_row()
+        for h in range(2):
+            d_pass(h, 0, 0)
 
     with scope("gather_far_e"):
         gather_far(1, (0, 2, 3, 1))
         exch = exch + use(1, c, REST)
     with scope("gather_y_d"):
-        gather_y(0)
+        d_gather_row()
+    with scope("gather_0_d"):
+        d_gather_near((0,))
+        d_gather_far((0,))
     with scope("gather_core_e"):
         gather_core(1, 0)
         gather_core(1, 1)
         exch = exch + use(1, 1 - c, ROW + REST)
         near = gap * basis[R, :] + 2.0 * exch
         late_near = exact(near, basis[...], NT)
-
     with scope("gram_d"):
         part = None
         for m, j in ((0, 3), (1, 0), (2, 2), (3, 1)):
-            term = nt(gat[0, gat_block(0, m, 0, c)], qb[j])
+            term = nt(gat[0, d_block(0, m, 0, c)], qb[j])
             part = term if part is None else part + term
-        share(late, lx, ly, 0, late_near - part)
-        direct = use(0, c, ROW)
+        share_late(0, late_near - part)
+    with scope("gather_near_d"):
+        d_gather_near((2, 3, 1))
+    with scope("late1"):
+        share_late(1, late_sum(0))
+    with scope("gather_far_d"):
+        d_gather_far((1, 2, 3))
+    with scope("rest_d"):
+        direct = use(0, c, ROW + REST)
     with scope("early3"):
-        share(early, ex, ey, 3, shared(early, ey, 2))
-    with scope("core_row_d"):
-        gather_core(0, 0)
-        direct = direct + use(0, 1 - c, ROW)
-    with scope("late1"):
-        share(late, lx, ly, 1, shared(late, ly, 0))
-    with scope("gather_near_d"):
-        gather_near(0)
-    with scope("gather_far_d"):
-        gather_far(0, (0, 2))
+        share_early(3, early_sum(2))
+    with scope("gather_core_d"):
+        for h in range(2):
+            landed(gat.at[0, pl.ds(0, 16), :, HALF[h]], a3y.at[0, h])
+        direct = direct + use(0, 1 - c, ROW + REST)
     with scope("late2"):
-        share(late, lx, ly, 2, shared(late, ly, 1))
-    with scope("gather_far2_d"):
-        gather_far(0, (3, 1))
-    with scope("rest_d"):
-        direct = direct + use(0, c, REST)
-        gram = shared(early, ey, 3)
-    with scope("gather_core_d"):
-        gather_core(0, 1)
-        direct = direct + use(0, 1 - c, REST)
-    with scope("late3"):
-        share(late, lx, ly, 3, shared(late, ly, 2))
+        share_late(2, late_sum(1))
     with scope("image"):
         images[R, :] = near - direct
         o_trial_img[...] = exact(all_coef, images[...])
         o_search_img[...] = exact(lower, images[...])
-        store(2, o_trial_img, h_trial_img)
-        store(3, o_search_img, h_search_img)
     with scope("late4"):
-        mid = shared(late, ly, 3)
+        mid = late_sum(2)
+        gram = early_sum(3)
         gram = jnp.concatenate([gram[0:NE], mid, gram[NE:2 * NE]], axis=0)
         o_gram[...] = jnp.transpose(gram)
-        store(4, o_gram, h_gram)
 
     with jax.named_scope("drain"):
         for i, ref in enumerate((
-            s0s, rls, s1s, s2s, s3r, seen.at[0], c0s, c1s, c2r,
-            gat.at[0, pl.ds(0, 31)], gat.at[1, pl.ds(0, 31)],
+            s0s, gat.at[:, pl.ds(0, 30)], gat.at[0, pl.ds(0, 19)], gat.at[1, pl.ds(0, 31)],
+            gat.at[0, pl.ds(0, 31), :, HALF[0]], gat.at[0, pl.ds(0, 31), :, HALF[1]],
+            early.at[0, 0], early.at[pl.ds(0, 3), pl.ds(0, 3)],
+            late.at[pl.ds(0, 7)], late.at[pl.ds(0, 6)],
         )):
             left(ref, sx.at[i])
-        for i in range(4):
-            count = 1 if i == 0 else 3
-            left(early.at[i, pl.ds(0, count)], ex.at[i])
-            left(late.at[i, pl.ds(0, count)], lx.at[i])
-        for copy in stores:
-            copy.wait()
 
 
 def put(*refs):
@@ -500,11 +563,11 @@
         args = (trial.T, resid.T, search.T, trial_img.T, search_img.T, dens_e, dens_d, screen,
                 coulomb.reshape(1, -1), val_e.reshape(1, -1), con_e.reshape(1, -1),
                 val_i.reshape(1, -1), con_i.reshape(1, -1), ritz.T)
+        args = tuple(pltpu.with_memory_space_constraint(a, pltpu.HBM) for a in args)
         dma = pltpu.SemaphoreType.DMA
         block = (NE, COLS)
         tall = pltpu.VMEM((3 * NE, ROWS), F32)
-        flat = pltpu.VMEM((NE, ROWS), F32)
-        scratch = [flat, flat, flat, flat, pltpu.VMEM((3 * NE, 3 * NE), F32), tall, tall] + [pltpu.VMEM(a.shape, a.dtype) for a in args[5:]] + [
+        scratch = [tall, tall] + [pltpu.VMEM(a.shape, a.dtype) for a in args[5:]] + [
             pltpu.VMEM((3 * NE, ROWS), BF16),
             pltpu.VMEM((5, 4, 4) + block, BF16),
             pltpu.VMEM((5, 4, 4) + block, BF16),
@@ -528,22 +591,22 @@
             pltpu.VMEM((3,) + block, BF16),
             pltpu.VMEM((2, 32) + block, BF16),
             pltpu.VMEM((4, 4, 2 * NE, 3 * NE), F32),
-            pltpu.VMEM((4, 4, NE, 3 * NE), F32),
-            dma((14,)), dma((5,)), dma((11,)), dma((4,)), dma((4,)),
+            pltpu.VMEM((16, NE, 3 * NE), F32),
+            dma((12,)), dma((10,)),
             dma((2, 4)), dma((3,)), dma((2, 4)), dma((3,)), dma((2, 2, 4)), dma((3,)),
             dma((2,)), dma((2,)), dma, dma((2,)), dma, dma,
-            dma((2, 3)), dma((2, 3, 4)), dma((2, 2)), dma((4,)), dma((4,)),
+            dma((3, 3)), dma((3, 3, 4)), dma((2, 2)), dma((4,)), dma((3,)),
         ]
         vec = jax.ShapeDtypeStruct((NE, ROWS), F32)
         outs = (vec, vec, vec, vec, jax.ShapeDtypeStruct((3 * NE, 3 * NE), F32))
         parts = pl.pallas_call(
             kernel,
-            out_shape=outs,
+            out_shape=tuple(pltpu.VMEM(o.shape, F32) for o in outs),
             in_specs=[pl.BlockSpec(memory_space=pl.ANY)] * len(args),
-            out_specs=[pl.BlockSpec(memory_space=pl.ANY)] * 5,
+            out_specs=[pl.BlockSpec(memory_space=pltpu.VMEM)] * 5,
             scratch_shapes=scratch,
             compiler_params=pltpu.CompilerParams(
-                collective_id=0, has_side_effects=True, vmem_limit_bytes=67043328
+                collective_id=0, has_side_effects=True, vmem_limit_bytes=56 * 1024 * 1024
             ),
             name="step",
         )(*args)
@@ -553,7 +616,7 @@
             in_specs=[pl.BlockSpec(memory_space=pltpu.VMEM)] * 5,
             out_specs=[pl.BlockSpec(memory_space=pl.ANY)] * 5,
             scratch_shapes=[dma((5,))],
-            compiler_params=pltpu.CompilerParams(vmem_limit_bytes=67043328),
+            compiler_params=pltpu.CompilerParams(vmem_limit_bytes=1024 * 1024),
             name="put",
         )(*parts)
         return tuple(a.T for a in parts[:4]) + (parts[4],)

time: 57.2 us -> 54.6 us (0.955)
  Pallas kernels: 56.4 us -> 53.8 us
    pallas_call x1, Pallas kernels: 54.9 us -> 53.1 us  [body(): pl.pallas_call(kernel, out_shape=tuple((pltpu.VMEM(o.shape, F32) for o in...]
    pallas_call x1, Pallas kernels: 1.51 us -> 0.68 us  [body(): pl.pallas_call(put, out_shape=outs, in_specs=[pl.BlockSpec(memory_space=p...]
where the time goes in v3:
time: 54.6 us; the launch traced here: 54.4 us
  Pallas kernels  53.8 us (99%)
  between operations  0.65 us (1%)
    pallas_call x1, Pallas kernels, body(): pl.pallas_call(kernel, out_shape=tuple((pltpu.VMEM(o.shape, F32) for o in...  53.1 us

profile of v3, /device:TPU:0, one launch (start us, length us, event | category | flops | bytes accessed | tf_op | source)
XLA Modules:
  0.0 54.4 jit_solution(14774285427663095368)
XLA Ops:
  0.6 53.1 %step.1 = (f32[24,48]{1,0:T(8,128)S(1)}, f32[24,48]{1,0:T(8,128)S(1)}, f32[24,48]{1,0:T(8,128)S(1)}, f32[24,48]{1,0:T(8,128)S(1)}, f32[72,72]{1,0:T(8,128)S(1)}) custom-call(f32[24,48]{1,0:T(8,128)} %bitcast.16, f32[24,48]{1,0:T(8,128)} %bitcast.17, f32[24,48]{1,0:T(8,128)} %bitcast.18, f32[24,48]{1,0:T(8,128)} %bitcast.19, f32[24,48]{1,0:T(8,128)} %bitcast.20, ...), custom_call_target="tpu_custom_call" | custom-call | tf_op jit(solution)/shard_map/step/pallas_call | solution.py:602
  53.7 0.7 %put.1 = (f32[24,48]{1,0:T(8,128)}, f32[24,48]{1,0:T(8,128)}, f32[24,48]{1,0:T(8,128)}, f32[24,48]{1,0:T(8,128)}, f32[72,72]{1,0:T(8,128)}) custom-call(f32[24,48]{1,0:T(8,128)S(1)} %get-tuple-element.15.refs_0_, f32[24,48]{1,0:T(8,128)S(1)} %get-tuple-element.16.refs_1_, f32[24,48]{1,0:T(8,128)S(1)} %get-tuple-element.17.refs_2_, ...), custom_call_target="tpu_custom_call" | custom-call | tf_op jit(solution)/shard_map/put/pallas_call | solution.py:613

commit v4 on v3

--- a/solution.py
+++ b/solution.py
@@ -39,8 +39,8 @@
     o_trial, o_trial_img, o_search, o_search_img, o_gram,
     basis, images, dens_e, dens_d, screen, coulomb, val_e, con_e, val_i, con_i, ritz,
     rt, s0s, s0r, acc, rls, rlr, s1s, s1r, s2s, s2r, s3s, s3r,
-    qb, seen, bacc, c0s, c0r, c1s, c1r, c2s, c2r, gat, early, late,
-    ld, sx, s0y, s0q, rly, rlq, s1y, s1q, s2y, s3y, s4y, c0y, c1y, c2y,
+    qb, seen, bacc, c0s, c0r, c2s, c2r, gat, early, late,
+    ld, sx, s0y, s0q, rly, rlq, s1y, s1q, s2y, s3y, s4y, c0y, c2y,
     a1y, a2y, a3y, ey, ly,
 ):
     blk = lax.axis_index("blk")
@@ -81,7 +81,7 @@
         pltpu.make_async_copy(two, two, sem).wait()
 
     barrier = pltpu.get_barrier_semaphore()
-    peers = [other] + [along(a, d) for a in "xyz" for d in FAR]
+    peers = [other, device(y=(y + 2) % 4, c=1 - c)] + [along(a, d) for a in "xyz" for d in FAR]
     peers += [device(x=(x + d) % 4, c=1 - c) for d in FAR]
     for peer in peers:
         pl.semaphore_signal(barrier, inc=1, device_id=peer, device_id_type=MESH)
@@ -425,33 +425,24 @@
         loads[4].wait()
         mine = gat_block(1, 0, 0, c)
         gat[1, mine] = (coulomb[:, lanes(mine)] * tot).astype(BF16)
+        pass_on(1, 0, 0)
     with scope("mm_far"):
         landed(seen.at[1 - y_lo], s4y)
-        kept = []
-        for i in (1, 0, 3, 2):
-            core = c if i > 1 else 1 - c
-            half = y_hi if i in (0, 2) else 1 - y_hi
+        across = (other, along("y", 2), device(y=(y + 2) % 4, c=1 - c))
+        for i in (2, 1, 0, 3):
+            core = c if i in (1, 3) else 1 - c
+            half = y_hi if i in (0, 3) else 1 - y_hi
             q = core * 2 + half
             rows = pl.ds(pl.multiple_of(q * COLS, COLS), COLS)
             v = bacc[q] + nt(seen[1 - y_lo], screen[rows, lanes(1 - y_lo)])
-            if i > 1:
-                kept.append(v)
+            if i == 3:
+                home = v
             else:
                 c0s[i] = v.astype(BF16)
-                send(c0s.at[i], c0r.at[i], sx.at[2], c0y.at[i], other)
-        away, home = kept
-        pass_on(1, 0, 0)
+                send(c0s.at[i], c0r.at[i], sx.at[2], c0y, across[i])
     with scope("rows_x"):
         gram_rows(2)
 
-    with scope("c0"):
-        for i in (1, 0):
-            landed(c0r.at[i], c0y.at[i])
-            if i == 1:
-                c1s[...] = (away + c0r[1].astype(F32)).astype(BF16)
-                send(c1s, c1r, sx.at[2], c1y, along("y", 2))
-            else:
-                home = home + c0r[0].astype(F32)
     with scope("relay_s"):
         relay(4)
         share_early(2, early_sum(1))
@@ -461,8 +452,9 @@
         gram_rows(3)
 
     with scope("c1"):
-        landed(c1r, c1y)
-        home = home + c1r[...].astype(F32)
+        landed(c0r, c0y)
+        for i in range(3):
+            home = home + c0r[i].astype(F32)
         c2s[...] = home.astype(BF16)
         for k in (0, 2, 1):
             send(c2s, c2r.at[k], sx.at[2], c2y, along("x", FAR[k]))
@@ -583,10 +575,8 @@
             pltpu.VMEM((4, 3 * NE, COLS), BF16),
             pltpu.VMEM((2,) + block, BF16),
             pltpu.VMEM((4,) + block, F32),
-            pltpu.VMEM((2,) + block, BF16),
-            pltpu.VMEM((2,) + block, BF16),
-            pltpu.VMEM(block, BF16),
-            pltpu.VMEM(block, BF16),
+            pltpu.VMEM((3,) + block, BF16),
+            pltpu.VMEM((3,) + block, BF16),
             pltpu.VMEM(block, BF16),
             pltpu.VMEM((3,) + block, BF16),
             pltpu.VMEM((2, 32) + block, BF16),
@@ -594,7 +584,7 @@
             pltpu.VMEM((16, NE, 3 * NE), F32),
             dma((12,)), dma((10,)),
             dma((2, 4)), dma((3,)), dma((2, 4)), dma((3,)), dma((2, 2, 4)), dma((3,)),
-            dma((2,)), dma((2,)), dma, dma((2,)), dma, dma,
+            dma((2,)), dma((2,)), dma, dma, dma,
             dma((3, 3)), dma((3, 3, 4)), dma((2, 2)), dma((4,)), dma((3,)),
         ]
         vec = jax.ShapeDtypeStruct((NE, ROWS), F32)

time: 54.6 us -> 52.8 us (0.967)
  Pallas kernels: 53.8 us -> 52 us
    pallas_call x1, Pallas kernels: 53.1 us -> 51.3 us  [body(): pl.pallas_call(kernel, out_shape=tuple((pltpu.VMEM(o.shape, F32) for o in...]
where the time goes in v4:
time: 52.8 us; the launch traced here: 52.6 us
  Pallas kernels  52 us (98%)
  between operations  0.65 us (1%)
    pallas_call x1, Pallas kernels, body(): pl.pallas_call(kernel, out_shape=tuple((pltpu.VMEM(o.shape, F32) for o in...  51.3 us

profile of v4, /device:TPU:0, one launch (start us, length us, event | category | flops | bytes accessed | tf_op | source)
XLA Modules:
  0.0 52.6 jit_solution(13582684043554967762)
XLA Ops:
  0.6 51.3 %step.1 = (f32[24,48]{1,0:T(8,128)S(1)}, f32[24,48]{1,0:T(8,128)S(1)}, f32[24,48]{1,0:T(8,128)S(1)}, f32[24,48]{1,0:T(8,128)S(1)}, f32[72,72]{1,0:T(8,128)S(1)}) custom-call(f32[24,48]{1,0:T(8,128)} %bitcast.16, f32[24,48]{1,0:T(8,128)} %bitcast.17, f32[24,48]{1,0:T(8,128)} %bitcast.18, f32[24,48]{1,0:T(8,128)} %bitcast.19, f32[24,48]{1,0:T(8,128)} %bitcast.20, ...), custom_call_target="tpu_custom_call" | custom-call | tf_op jit(solution)/shard_map/step/pallas_call | solution.py:592
  52.0 0.7 %put.1 = (f32[24,48]{1,0:T(8,128)}, f32[24,48]{1,0:T(8,128)}, f32[24,48]{1,0:T(8,128)}, f32[24,48]{1,0:T(8,128)}, f32[72,72]{1,0:T(8,128)}) custom-call(f32[24,48]{1,0:T(8,128)S(1)} %get-tuple-element.15.refs_0_, f32[24,48]{1,0:T(8,128)S(1)} %get-tuple-element.16.refs_1_, f32[24,48]{1,0:T(8,128)S(1)} %get-tuple-element.17.refs_2_, ...), custom_call_target="tpu_custom_call" | custom-call | tf_op jit(solution)/shard_map/put/pallas_call | solution.py:603

commit v5 on v4

--- a/solution.py
+++ b/solution.py
@@ -41,7 +41,7 @@
     rt, s0s, s0r, acc, rls, rlr, s1s, s1r, s2s, s2r, s3s, s3r,
     qb, seen, bacc, c0s, c0r, c2s, c2r, gat, early, late,
     ld, sx, s0y, s0q, rly, rlq, s1y, s1q, s2y, s3y, s4y, c0y, c2y,
-    a1y, a2y, a3y, ey, ly,
+    a1y, a2y, d2y, a3y, ey, ly,
 ):
     blk = lax.axis_index("blk")
     grp = lax.axis_index("grp")
@@ -173,7 +173,7 @@
     def ring(p, way, j, v):
         s1s[p, way, j] = v.astype(BF16)
         send(s1s.at[p, way, j], s1r.at[p, way, j], sx.at[1],
-             s1q.at[p - 2] if p > 1 else s1y.at[p, way, j], along(first[p], (1, 3)[way]))
+             s1q.at[p - 2] if p > 1 else s1y.at[p, j], along(first[p], (1, 3)[way]))
 
     def relay(p):
         if p > 1:
@@ -187,8 +187,8 @@
     def second_axis(p):
         for j in (0, 2, 1, 3):
             v = acc[p, 3, j]
+            landed(s1r.at[p, :, j], s1y.at[p, j])
             for way in range(2):
-                landed(s1r.at[p, way, j], s1y.at[p, way, j])
                 v = v + s1r[p, way, j].astype(F32)
             if j == 3:
                 acc[p, 3, j] = v
@@ -240,11 +240,11 @@
             for k in (0, 2, 1):
                 send(ref, ref, sx.at[3], a1y.at[p, k], along(row[p], FAR[k]))
         if kz == 0:
-            send(ref, ref, sx.at[3], a2y.at[p, 1, m], along(col[p], 3))
-        if (kz == 0 and m % 2 == 1) or (kz == 2 and m % 2 == 0):
-            send(ref, ref, sx.at[3], a2y.at[p, 2, m], along(col[p], 2 if kz == 0 else 3))
+            send(ref, ref, sx.at[3], a2y.at[1, m], along(col[p], 3))
+        if (kz == 1 and m % 2 == 1) or (kz == 2 and m % 2 == 0):
+            send(ref, ref, sx.at[3], a2y.at[2, m], along(col[p], 1 if kz == 1 else 3))
         if kz == 0:
-            send(ref, ref, sx.at[3], a2y.at[p, 0, m], along(col[p], 1))
+            send(ref, ref, sx.at[3], a2y.at[0, m], along(col[p], 1))
 
     def use(p, core, pairs):
         term = None
@@ -265,12 +265,12 @@
     def gather_near(p):
         for m in (0, 2, 3, 1):
             for kz in (2, 1):
-                landed(gat.at[p, gat_block(p, m, kz, c)], a2y.at[p, kz - 1, m])
+                landed(gat.at[p, gat_block(p, m, kz, c)], a2y.at[kz - 1, m])
                 pass_on(p, m, kz)
 
     def gather_far(p, which):
         for m in which:
-            landed(gat.at[p, gat_block(p, m, 3, c)], a2y.at[p, 2, m])
+            landed(gat.at[p, gat_block(p, m, 3, c)], a2y.at[2, m])
             pass_on(p, m, 3)
 
     def gather_core(p, rest):
@@ -293,36 +293,36 @@
         for k in (0, 2, 1):
             for h in range(2):
                 ref = d_ref(h, 0, 0)
-                send(ref, ref, sx.at[4 + h], a1y.at[2 * h, k], along(ROWS2[h], FAR[k]))
+                send(ref, ref, sx.at[4 + h], a1y.at[0, k], along(ROWS2[h], FAR[k]))
 
     def d_pass(h, m, kz):
         ref = d_ref(h, m, kz)
         ssem = sx.at[4 + h]
         send(ref, ref, ssem, a3y.at[0, h], other)
         if kz == 0:
-            send(ref, ref, ssem, a2y.at[2 * h, 1, m], along(COLS2[h], 3))
-        if (kz == 0 and m < 2) or (kz == 2 and m > 1):
-            send(ref, ref, ssem, a2y.at[2 * h, 2, m], along(COLS2[h], 2 if kz == 0 else 3))
+            send(ref, ref, ssem, d2y.at[h, m], along(COLS2[h], 3))
         if kz == 0:
-            send(ref, ref, ssem, a2y.at[2 * h, 0, m], along(COLS2[h], 1))
+            send(ref, ref, ssem, d2y.at[2, m], along(COLS2[h], 2 if kz == 0 else 3))
+        if kz == 0:
+            send(ref, ref, ssem, d2y.at[h, m], along(COLS2[h], 1))
 
     def d_gather_row():
         for m in (2, 3, 1):
+            landed(gat.at[0, 0], a1y.at[0, m - 1])
             for h in range(2):
-                landed(d_ref(h, m, 0), a1y.at[2 * h, m - 1])
                 d_pass(h, m, 0)
 
     def d_gather_near(which):
         for m in which:
             for h in range(2):
+                landed(gat.at[0, pl.ds(0, 2), :, HALF[h]], d2y.at[h, m])
                 for kz in (2, 1):
-                    landed(d_ref(h, m, kz), a2y.at[2 * h, kz - 1, m])
                     d_pass(h, m, kz)
 
     def d_gather_far(which):
         for m in which:
+            landed(gat.at[0, 0], d2y.at[2, m])
             for h in range(2):
-                landed(d_ref(h, m, 3), a2y.at[2 * h, 2, m])
                 d_pass(h, m, 3)
 
     def spread(buf, sem, ssem, here, value, devices):
@@ -583,9 +583,9 @@
             pltpu.VMEM((4, 4, 2 * NE, 3 * NE), F32),
             pltpu.VMEM((16, NE, 3 * NE), F32),
             dma((12,)), dma((10,)),
-            dma((2, 4)), dma((3,)), dma((2, 4)), dma((3,)), dma((2, 2, 4)), dma((3,)),
+            dma((2, 4)), dma((3,)), dma((2, 4)), dma((3,)), dma((2, 4)), dma((3,)),
             dma((2,)), dma((2,)), dma, dma, dma,
-            dma((3, 3)), dma((3, 3, 4)), dma((2, 2)), dma((4,)), dma((3,)),
+            dma((2, 3)), dma((3, 4)), dma((3, 4)), dma((2, 2)), dma((4,)), dma((3,)),
         ]
         vec = jax.ShapeDtypeStruct((NE, ROWS), F32)
         outs = (vec, vec, vec, vec, jax.ShapeDtypeStruct((3 * NE, 3 * NE), F32))

time: 52.8 us -> 52.4 us (level)
  no operation moved by 1% of the time
where the time goes in v5:
time: 52.4 us; the launch traced here: 52.2 us
  Pallas kernels  51.6 us (98%)
  between operations  0.65 us (1%)
    pallas_call x1, Pallas kernels, body(): pl.pallas_call(kernel, out_shape=tuple((pltpu.VMEM(o.shape, F32) for o in...  50.9 us

profile of v5, /device:TPU:0, one launch (start us, length us, event | category | flops | bytes accessed | tf_op | source)
XLA Modules:
  0.0 52.2 jit_solution(11728962129664109076)
XLA Ops:
  0.6 50.9 %step.1 = (f32[24,48]{1,0:T(8,128)S(1)}, f32[24,48]{1,0:T(8,128)S(1)}, f32[24,48]{1,0:T(8,128)S(1)}, f32[24,48]{1,0:T(8,128)S(1)}, f32[72,72]{1,0:T(8,128)S(1)}) custom-call(f32[24,48]{1,0:T(8,128)} %bitcast.16, f32[24,48]{1,0:T(8,128)} %bitcast.17, f32[24,48]{1,0:T(8,128)} %bitcast.18, f32[24,48]{1,0:T(8,128)} %bitcast.19, f32[24,48]{1,0:T(8,128)} %bitcast.20, ...), custom_call_target="tpu_custom_call" | custom-call | tf_op jit(solution)/shard_map/step/pallas_call | solution.py:592
  51.5 0.7 %put.1 = (f32[24,48]{1,0:T(8,128)}, f32[24,48]{1,0:T(8,128)}, f32[24,48]{1,0:T(8,128)}, f32[24,48]{1,0:T(8,128)}, f32[72,72]{1,0:T(8,128)}) custom-call(f32[24,48]{1,0:T(8,128)S(1)} %get-tuple-element.15.refs_0_, f32[24,48]{1,0:T(8,128)S(1)} %get-tuple-element.16.refs_1_, f32[24,48]{1,0:T(8,128)S(1)} %get-tuple-element.17.refs_2_, ...), custom_call_target="tpu_custom_call" | custom-call | tf_op jit(solution)/shard_map/put/pallas_call | solution.py:603

commit v6 on v5

--- a/solution.py
+++ b/solution.py
@@ -486,15 +486,16 @@
     with scope("gather_far_e"):
         gather_far(1, (0, 2, 3, 1))
         exch = exch + use(1, c, REST)
+        gather_core(1, 0)
+        exch = exch + use(1, 1 - c, ROW)
     with scope("gather_y_d"):
         d_gather_row()
     with scope("gather_0_d"):
         d_gather_near((0,))
         d_gather_far((0,))
     with scope("gather_core_e"):
-        gather_core(1, 0)
         gather_core(1, 1)
-        exch = exch + use(1, 1 - c, ROW + REST)
+        exch = exch + use(1, 1 - c, REST)
         near = gap * basis[R, :] + 2.0 * exch
         late_near = exact(near, basis[...], NT)
     with scope("gram_d"):

time: 52.4 us -> 52.3 us (level)
  no operation moved by 1% of the time
where the time goes in v6:
time: 52.3 us; the launch traced here: 52.1 us
  Pallas kernels  51.5 us (98%)
  between operations  0.65 us (1%)
    pallas_call x1, Pallas kernels, body(): pl.pallas_call(kernel, out_shape=tuple((pltpu.VMEM(o.shape, F32) for o in...  50.8 us

profile of v6, /device:TPU:0, one launch (start us, length us, event | category | flops | bytes accessed | tf_op | source)
XLA Modules:
  0.0 52.1 jit_solution(14258944012102026160)
XLA Ops:
  0.6 50.8 %step.1 = (f32[24,48]{1,0:T(8,128)S(1)}, f32[24,48]{1,0:T(8,128)S(1)}, f32[24,48]{1,0:T(8,128)S(1)}, f32[24,48]{1,0:T(8,128)S(1)}, f32[72,72]{1,0:T(8,128)S(1)}) custom-call(f32[24,48]{1,0:T(8,128)} %bitcast.16, f32[24,48]{1,0:T(8,128)} %bitcast.17, f32[24,48]{1,0:T(8,128)} %bitcast.18, f32[24,48]{1,0:T(8,128)} %bitcast.19, f32[24,48]{1,0:T(8,128)} %bitcast.20, ...), custom_call_target="tpu_custom_call" | custom-call | tf_op jit(solution)/shard_map/step/pallas_call | solution.py:593
  51.4 0.7 %put.1 = (f32[24,48]{1,0:T(8,128)}, f32[24,48]{1,0:T(8,128)}, f32[24,48]{1,0:T(8,128)}, f32[24,48]{1,0:T(8,128)}, f32[72,72]{1,0:T(8,128)}) custom-call(f32[24,48]{1,0:T(8,128)S(1)} %get-tuple-element.15.refs_0_, f32[24,48]{1,0:T(8,128)S(1)} %get-tuple-element.16.refs_1_, f32[24,48]{1,0:T(8,128)S(1)} %get-tuple-element.17.refs_2_, ...), custom_call_target="tpu_custom_call" | custom-call | tf_op jit(solution)/shard_map/put/pallas_call | solution.py:604
